TPU v7x, 32 devices: a whole 2x2x4 slice. The times are simulated.
32 devices in a mesh: rep: 8 (over y, x, core), shard: 4 (over z).
Axes of the slice: x: 2, y: 2, z: 4, core: 2. Of those that a mesh axis runs over, the one named last changes fastest.
Arguments:
- tokens: bfloat16 [64, 512, 768], P(('rep', 'shard')), may hold values from -6 to 6
- segment_ids: int32 [64, 512], P(('rep', 'shard')), may hold values from 0 to 63, never falling along the last dimension, each value on 1 to 256 neighbouring positions
- norm_gain: bfloat16 [768], P('shard'), may hold values from 0.5 to 1.5
- in_weight: bfloat16 [768, 3352], P('shard'), may hold values from -0.21875 to 0.21875
- conv_weight: bfloat16 [1792, 4], P('shard'), may hold values from -3 to 3
- conv_bias: bfloat16 [1792], P('shard'), may hold values from -3 to 3
- dt_bias: float32 [24], replicated, may hold values from -5 to -1
- a_log: float32 [24], replicated, may hold values from 0 to 2.77
- d_skip: float32 [24], replicated, may hold values from 0.5 to 1.5
- gate_gain: bfloat16 [1536], P('shard'), may hold values from 0.5 to 1.5
- out_weight: bfloat16 [1536, 768], P('shard'), may hold values from -0.15625 to 0.15625
- cotangent: bfloat16 [64, 512, 768], P(('rep', 'shard')), may hold values from -6 to 6
Outputs:
- mixed: bfloat16 [64, 512, 768], P(('rep', 'shard'))
- grad_tokens: float32 [64, 512, 768], P(('rep', 'shard'))
- grad_norm_gain: float32 [768], P('shard')
- grad_in_weight: float32 [768, 3352], P('shard')
- grad_conv_weight: float32 [1792, 4], P('shard')
- grad_conv_bias: float32 [1792], P('shard')
- grad_dt_bias: float32 [24], replicated
- grad_a_log: float32 [24], replicated
- grad_d_skip: float32 [24], replicated
- grad_gate_gain: float32 [1536], P('shard')
- grad_out_weight: float32 [1536, 768], P('shard')
Inputs may be any that keep to these rules, and one draw needn't show every extreme that they name: `segment_ids`: along each sequence the segment numbers never fall, so every document is a run of consecutive tokens; the longest run in a sequence has at most 256 tokens.
All inputs are finite; a program needn't handle non-finite values.
Results may differ from a plain program's by a relative error of at most 0.0073.
Values may be sent and summed in bfloat16 or wider, within the bound.
A program may use at most 256 MiB of HBM per device.

v0:
```python
from functools import partial

import jax
import jax.numpy as jnp
from jax import lax
from jax.experimental import pallas as pl
from jax.experimental.pallas import tpu as pltpu
from jax.sharding import PartitionSpec as P

HEADS = 24
HEADDIM = 64
STATE = 128
CONV = 4
INNER = 1536
CONV_CH = 1792
MODEL = 768
PROJ = 3352
PADDED = 3456
EPS = 1e-05

LEN = 512
CHUNK = 128
SEQ = 2
TOKENS = SEQ * LEN
QUADS = INNER // 256

f32 = jnp.float32
bf16 = jnp.bfloat16


def nn(a, b):
    return lax.dot_general(a, b, (((1,), (0,)), ((), ())), preferred_element_type=f32)


def nt(a, b):
    return lax.dot_general(a, b, (((1,), (1,)), ((), ())), preferred_element_type=f32)


def tn(a, b):
    return lax.dot_general(a, b, (((0,), (0,)), ((), ())), preferred_element_type=f32)


def exact(a, b):
    return lax.dot_general(
        a, b, (((1,), (0,)), ((), ())), preferred_element_type=f32, precision=lax.Precision.HIGHEST
    )


def sigmoid(v):
    return 0.5 * jnp.tanh(0.5 * v) + 0.5


def partial_sum(a):
    return a.reshape(a.shape[0] // 8, 8, a.shape[1]).sum(axis=0)


def lanes_of(shape):
    return lax.broadcasted_iota(jnp.int32, shape, 1)


def rows_of(shape):
    return lax.broadcasted_iota(jnp.int32, shape, 0)


def packed(a):
    a = jnp.where(lanes_of(a.shape) < HEADS, a, 0.0)
    high = a.astype(bf16).astype(f32)
    rest = a - high
    middle = rest.astype(bf16).astype(f32)
    low = rest - middle
    return (high + pltpu.roll(middle, 32, 1) + pltpu.roll(low, 64, 1)).astype(bf16)


def two_parts(a):
    high = a.astype(bf16)
    return high, (a - high.astype(f32)).astype(bf16)


def y_at(row, count, cols):
    right = cols.start >= MODEL
    base, shift = (LEN, MODEL) if right else (0, 0)
    return pl.ds(pl.multiple_of(base + row, 8), count), slice(cols.start - shift, cols.stop - shift)


def setup(seg_ref, win, s):
    r, c = rows_of((128, 256)), lanes_of((128, 256))
    for j in range(HEADS * 128 // 256):
        s["one128"][:, j * 256 : (j + 1) * 256] = (
            ((r & 31) == ((c + j * 256) >> 7)) & (r < 96)
        ).astype(f32).astype(bf16)
    for j in range(QUADS):
        s["one64"][:, j * 256 : (j + 1) * 256] = (
            ((r & 31) == ((c + j * 256) >> 6)) & (r < 96)
        ).astype(f32).astype(bf16)
    r, c = rows_of((256, 128)), lanes_of((256, 128))
    for j in range(QUADS):
        s["sum64"][j * 256 : (j + 1) * 256, :] = (((r + j * 256) >> 6) == c).astype(f32).astype(bf16)
    s["wdt"][...] = jnp.zeros((MODEL, 128), bf16)
    s["wdt"][:, :HEADS] = win[:, INNER + CONV_CH : PROJ]
    s["acc"][...] = jnp.zeros(s["acc"].shape, f32)
    s["pre"][TOKENS:, :] = jnp.zeros((16, CONV_CH), bf16)
    s["up"][:, 0:8, :] = jnp.zeros((2, 8, 256), f32)
    for q in range(SEQ):
        s["segc"][q, 0:8, :] = jnp.full((8, 128), -1.0, f32)
        for i in range(LEN // 128):
            seg = seg_ref[q : q + 1, i * 128 : (i + 1) * 128].astype(f32)
            s["segc"][q, 8 + i * 128 : 8 + (i + 1) * 128, :] = jnp.broadcast_to(seg, (128, 128)).T


def project(q, x_ref, seg_ref, win, sm, hd, s):
    row0 = pl.multiple_of(q * LEN, LEN)
    for i in range(LEN // 128):
        rows = pl.ds(row0 + i * 128, 128)
        x = x_ref[rows, :].astype(f32)
        r = lax.rsqrt(jnp.mean(x * x, axis=1, keepdims=True) + EPS)
        s["nrm"][rows, :] = (x * r * sm[6:7, :MODEL]).astype(bf16)
    seg = s["segc"][q, 8 : 8 + LEN, :]
    place = rows_of((LEN, 128))
    for o in range(1, CONV):
        s["back"][o - 1] = ((seg == pltpu.roll(seg, o, 0)) & (place >= o)).astype(f32)
    rows = pl.ds(row0, LEN)
    raw = nn(s["nrm"][rows, :], s["wdt"][...]) + hd[0:1, :]
    s["dtx"][rows, :] = raw
    for j in range(CONV_CH // 256):
        slot = j % 2
        s["up"][slot, 8:, :] = nn(s["nrm"][rows, :], win[:, INNER + j * 256 : INNER + (j + 1) * 256])
        for i in range(LEN // 128):
            for half in range(2):
                c0 = j * 256 + half * 128
                here = pl.ds(row0 + i * 128, 128)
                block = s["up"][slot, i * 128 : i * 128 + 136, half * 128 : (half + 1) * 128]
                u = block[8:]
                tap = lambda k: sm[k : k + 1, c0 : c0 + 128]
                pre = sm[4:5, c0 : c0 + 128] + tap(3) * u
                for o in range(1, CONV):
                    same = s["back"][o - 1, i * 128 : (i + 1) * 128, :]
                    pre = pre + tap(3 - o) * (pltpu.roll(block, o, 0)[8:] * same)
                s["u"][here, c0 : c0 + 128] = u.astype(bf16)
                s["pre"][here, c0 : c0 + 128] = pre.astype(bf16)
                s["xbc"][here, c0 : c0 + 128] = (pre * sigmoid(pre)).astype(bf16)


def chunk_terms(q, c, seg_ref, hd, s):
    row0 = pl.multiple_of(q * LEN + c * CHUNK, CHUNK)
    rows = pl.ds(row0, CHUNK)
    raw = s["dtx"][rows, :]
    dt = jnp.maximum(raw, 0.0) + jnp.log1p(jnp.exp(-jnp.abs(raw)))
    rate = -jnp.exp(hd[1:2, :]) * dt
    lower = (rows_of((CHUNK, CHUNK)) >= lanes_of((CHUNK, CHUNK))).astype(f32)
    cum = exact(lower, rate)
    source = cum - jnp.log(jnp.maximum(dt, 1e-37))
    start = 8 + c * CHUNK
    segc = s["segc"][q, pl.ds(pl.multiple_of(start, 8), CHUNK), :]
    segr = segc.T
    before = s["segc"][q, pl.ds(pl.multiple_of(start - 8, 8), 8), :][7:8]
    last = segc[CHUNK - 1 : CHUNK]
    carry = (segc == before).astype(f32)
    tail = (segc == last).astype(f32)
    end = cum[CHUNK - 1 : CHUNK, :]
    keep = jnp.exp(end) * (before == last).astype(f32)
    grow = jnp.exp(cum) * carry
    shrink = jnp.exp(end - source) * tail
    return rows, raw, dt, rate, cum, source, segc, segr, grow, shrink, keep


def scan_forward(q, c, seg_ref, sm, hd, s):
    rows, raw, dt, rate, cum, source, segc, segr, grow, shrink, keep = chunk_terms(q, c, seg_ref, hd, s)
    t, k = rows_of((CHUNK, CHUNK)), lanes_of((CHUNK, CHUNK))
    bound = jnp.where((segc == segr) & (t >= k), 3e38, -1e30)
    s["rowv"][...] = source.T
    target = packed(cum)
    grow_p, shrink_p = packed(grow), packed(shrink)
    keep_p = packed(jnp.broadcast_to(keep, (8, 128)))
    bv = s["xbc"][rows, INNER : INNER + STATE]
    cv = s["xbc"][rows, INNER + STATE :]
    gram = nt(cv, bv)
    bt = bv.T
    at = q * (LEN // CHUNK) + c
    left = lanes_of((CHUNK, 128)) < HEADDIM
    for j in range(QUADS):
        cols = slice(j * 256, (j + 1) * 256)
        grow_e = nn(grow_p, s["one64"][:, cols])
        shrink_e = nn(shrink_p, s["one64"][:, cols])
        keep_e = nn(keep_p, s["one64"][:, cols])[0:1, :]
        state = s["state"][:, cols]
        low_state = state.astype(bf16)
        s["states"][at, :, cols] = low_state
        y_state = nn(cv, low_state)
        xv = s["xbc"][rows, cols]
        xw = (xv.astype(f32) * shrink_e).astype(bf16)
        s["state"][:, cols] = state * keep_e + nn(bt, xw)
        parts = []
        for pair in range(2):
            spread = nn(target, s["one128"][:, j * 512 + pair * 256 : j * 512 + (pair + 1) * 256])
            weights = []
            for half in range(2):
                head = 4 * j + 2 * pair + half
                d = spread[:, half * 128 : (half + 1) * 128] - s["rowv"][head : head + 1, :]
                weights.append((gram * jnp.exp(jnp.minimum(d, bound))).astype(bf16))
            x2 = xv[:, pair * 128 : (pair + 1) * 128]
            zero = jnp.zeros_like(x2)
            stack = jnp.concatenate([jnp.where(left, x2, zero), jnp.where(left, zero, x2)], axis=0)
            parts.append(nn(jnp.concatenate(weights, axis=1), stack))
        s["y"][y_at(c * CHUNK, CHUNK, cols)] = (
            jnp.concatenate(parts, axis=1) + y_state * grow_e
        )


def gate(q, i, x_ref, cot_ref, win, wout, sm, mixed_ref, s):
    tall, block = 256, 64
    row0 = q * LEN + i * tall
    rows = pl.ds(pl.multiple_of(row0, tall), tall)
    for j in range(QUADS):
        cols = slice(j * 256, (j + 1) * 256)
        s["z"][:, cols] = nn(s["nrm"][rows, :], win[:, cols])
        s["dg"][:, cols] = nt(cot_ref[rows, :], wout[cols, :])

    @pl.loop(0, tall // block)
    def _(b):
        own = pl.ds(pl.multiple_of(b * block, block), block)
        here = i * tall + b * block
        where = pl.ds(pl.multiple_of(row0 + b * block, block), block)
        square = jnp.zeros((block, 128), f32)
        along = jnp.zeros((block, 128), f32)
        for j in range(INNER // 128):
            cols = slice(j * 128, (j + 1) * 128)
            z = s["z"][own, cols]
            y = s["y"][y_at(here, block, cols)] + sm[7:8, cols] * s["xbc"][where, cols].astype(f32)
            v = y * (z * sigmoid(z))
            square = square + v * v
            along = along + s["dg"][own, cols] * sm[5:6, cols] * v
        r = lax.rsqrt(jnp.sum(square, axis=1, keepdims=True) * (1.0 / INNER) + EPS)
        k = r * r * r * (jnp.sum(along, axis=1, keepdims=True) * (1.0 / INNER))
        for j in range(INNER // 128):
            cols = slice(j * 128, (j + 1) * 128)
            z = s["z"][own, cols]
            dg = s["dg"][own, cols]
            ys = s["y"][y_at(here, block, cols)]
            xv = s["xbc"][where, cols].astype(f32)
            y = ys + sm[7:8, cols] * xv
            sg = sigmoid(z)
            zs = z * sg
            v = y * zs
            vr = v * r
            gain = sm[5:6, cols]
            s["gated"][where, cols] = (vr * gain).astype(bf16)
            s["acc"][5, :, cols] += partial_sum(dg * vr)
            dv = r * (dg * gain) - v * k
            dy = dv * zs
            low_dy = dy.astype(bf16)
            s["dy"][where, cols] = low_dy
            s["dz"][where, cols] = (dv * y * (sg + zs * (1.0 - sg))).astype(bf16)
            s["acc"][7, :, cols] += partial_sum(dy * xv)
            s["dg"][own, cols] = low_dy.astype(f32) * ys

    high, low = two_parts(s["dg"][...])
    s["rowdot"][rows, :] = nn(high, s["sum64"][...]) + nn(low, s["sum64"][...])
    branch = nn(s["gated"][rows, :], wout[...])
    mixed_ref[rows, :] = (x_ref[rows, :].astype(f32) + branch).astype(bf16)


def scan_backward(q, c, seg_ref, sm, hd, s):
    rows, raw, dt, rate, cum, source, segc, segr, grow, shrink, keep = chunk_terms(q, c, seg_ref, hd, s)
    k, t = rows_of((CHUNK, CHUNK)), lanes_of((CHUNK, CHUNK))
    allowed = (segc == segr) & (t >= k)
    bound = jnp.where(allowed, 3e38, -1e30)
    s["rowv"][...] = cum.T
    origin = packed(source)
    grow_p, shrink_p = packed(grow), packed(shrink)
    keep_p = packed(jnp.broadcast_to(keep, (8, 128)))
    bv = s["xbc"][rows, INNER : INNER + STATE]
    cv = s["xbc"][rows, INNER + STATE :]
    gram = nt(bv, cv)
    ct = cv.T
    at = q * (LEN // CHUNK) + c
    left = lanes_of((CHUNK, 128)) < HEADDIM
    dgram = jnp.zeros((CHUNK, CHUNK), f32)
    for j in range(QUADS):
        cols = slice(j * 256, (j + 1) * 256)
        grow_e = nn(grow_p, s["one64"][:, cols])
        s["dys"][:, cols] = (s["dy"][rows, cols].astype(f32) * grow_e).astype(bf16)
        shrink_e = nn(shrink_p, s["one64"][:, cols])
        s["xw"][:, cols] = (s["xbc"][rows, cols].astype(f32) * shrink_e).astype(bf16)
        low_dstate = s["state"][:, cols].astype(bf16)
        s["lowd"][:, cols] = low_dstate
        part = nn(bv, low_dstate) * shrink_e
        s["part"][:, cols] = part
        keep_e = nn(keep_p, s["one64"][:, cols])[0:1, :]
        kept = s["state"][:, cols] * keep_e
        s["tail"][:, cols] = partial_sum(s["xbc"][rows, cols].astype(f32) * part) + partial_sum(
            kept * s["states"][at, :, cols].astype(f32)
        )
        s["state"][:, cols] = kept + nn(ct, s["dys"][:, cols])
    for j in range(INNER // 128):
        cols = slice(j * 128, (j + 1) * 128)
        xv = s["xbc"][rows, cols]
        dy = s["dy"][rows, cols]
        spread = nn(origin, s["one128"][:, j * 256 : (j + 1) * 256])
        zero = jnp.zeros_like(dy)
        stack = jnp.concatenate([jnp.where(left, dy, zero), jnp.where(left, zero, dy)], axis=0)
        dweights = nt(xv, stack)
        weights = []
        for half in range(2):
            head = 2 * j + half
            d = s["rowv"][head : head + 1, :] - spread[:, half * 128 : (half + 1) * 128]
            e = jnp.exp(jnp.minimum(d, bound))
            weights.append((gram * e).astype(bf16))
            dgram = dgram + dweights[:, half * 128 : (half + 1) * 128] * e
        dx = nn(jnp.concatenate(weights, axis=1), stack) + s["part"][:, cols]
        s["part"][:, cols] = xv.astype(f32) * dx
        dx = dx + sm[7:8, cols] * dy.astype(f32)
        pre = s["pre"][rows, cols].astype(f32)
        sg = sigmoid(pre)
        s["pre"][rows, cols] = (dx * (sg * (1.0 + pre * (1.0 - sg)))).astype(bf16)
    high, low = two_parts(s["part"][...])
    colsum = nn(high, s["sum64"][...]) + nn(low, s["sum64"][...])
    high, low = two_parts(s["tail"][...])
    dlast = jnp.sum(nn(high, s["sum64"][...]) + nn(low, s["sum64"][...]), axis=0, keepdims=True)
    dc = nt(s["dys"][...], s["states"][at])
    db = nt(s["xw"][...], s["lowd"][...])
    low_dgram = dgram.astype(bf16)
    db = db + nn(low_dgram, cv)
    dc = dc + tn(low_dgram, bv)
    for index, d in ((0, db), (1, dc)):
        cols = slice(INNER + index * STATE, INNER + (index + 1) * STATE)
        pre = s["pre"][rows, cols].astype(f32)
        sg = sigmoid(pre)
        s["pre"][rows, cols] = (d * (sg * (1.0 + pre * (1.0 - sg)))).astype(bf16)
    dcum = s["rowdot"][rows, :] - colsum
    drate = exact(allowed.astype(f32), dcum) + dlast * (segc == segc[CHUNK - 1 : CHUNK]).astype(f32)
    sg = sigmoid(raw)
    ratio = jnp.where(dt > 1e-30, sg / jnp.maximum(dt, 1e-30), 1.0)
    draw = colsum * ratio - drate * jnp.exp(hd[1:2, :]) * sg
    draw = jnp.where(lanes_of((CHUNK, 128)) < HEADS, draw, 0.0)
    s["ddt"][rows, :] = draw.astype(bf16)
    s["acc"][8, :, 0:128] += partial_sum(draw)
    s["acc"][9, :, 0:128] += partial_sum(drate * rate)


def conv_backward(q, sm, s):
    row0 = pl.multiple_of(q * LEN, LEN)
    rows = pl.ds(row0, LEN)
    seg = s["segc"][q, 8 : 8 + LEN, :]
    place = rows_of((LEN, 128))
    for o in range(1, CONV):
        s["back"][o - 1] = ((seg == pltpu.roll(seg, LEN - o, 0)) & (place < LEN - o)).astype(f32)
    for j in range(CONV_CH // 128):
        cols = slice(j * 128, (j + 1) * 128)
        sums = [jnp.zeros((8, 128), f32)] * 5
        for i in range(LEN // 128):
            here = pl.ds(row0 + i * 128, 128)
            block = s["pre"][pl.ds(row0 + i * 128, 144), cols].astype(f32)
            ds = block[:128]
            u = s["u"][here, cols].astype(f32)
            du = sm[3:4, cols] * ds
            sums[4] = sums[4] + partial_sum(ds)
            sums[3] = sums[3] + partial_sum(ds * u)
            for o in range(1, CONV):
                moved = pltpu.roll(block, 144 - o, 0)[:128] * s["back"][o - 1, i * 128 : (i + 1) * 128, :]
                du = du + sm[3 - o : 4 - o, cols] * moved
                sums[3 - o] = sums[3 - o] + partial_sum(moved * u)
            s["u"][here, cols] = du.astype(bf16)
        for k in range(5):
            s["acc"][k, :, cols] += sums[k]


def input_gradient(i, x_ref, cot_ref, sm, gtok_ref, s):
    rows = pl.ds(pl.multiple_of(i * 128, 128), 128)
    x = x_ref[rows, :].astype(f32)
    dn = gtok_ref[rows, :]
    r = lax.rsqrt(jnp.mean(x * x, axis=1, keepdims=True) + EPS)
    s["acc"][6, :, 0:MODEL] += partial_sum(dn * (x * r))
    h = dn * sm[6:7, :MODEL]
    k = r * r * r * jnp.mean(h * x, axis=1, keepdims=True)
    gtok_ref[rows, :] = r * h - k * x + cot_ref[rows, :].astype(f32)


SCRATCH = dict(
    nrm=((TOKENS, MODEL), bf16),
    u=((TOKENS, CONV_CH), bf16),
    pre=((TOKENS + 16, CONV_CH), bf16),
    xbc=((TOKENS, CONV_CH), bf16),
    dtx=((TOKENS, 128), f32),
    gated=((TOKENS, INNER), bf16),
    dy=((TOKENS, INNER), bf16),
    dz=((TOKENS, INNER), bf16),
    ddt=((TOKENS, 128), bf16),
    z=((256, INNER), f32),
    dg=((256, INNER), f32),
    rowdot=((TOKENS, 128), f32),
    dys=((CHUNK, INNER), bf16),
    xw=((CHUNK, INNER), bf16),
    lowd=((CHUNK, INNER), bf16),
    part=((CHUNK, INNER), f32),
    up=((2, 8 + LEN, 256), f32),
    state=((STATE, INNER), f32),
    states=((SEQ * LEN // CHUNK, STATE, INNER), bf16),
    rowv=((128, 128), f32),
    tail=((8, INNER), f32),
    segc=((SEQ, 8 + LEN, 128), f32),
    back=((CONV - 1, LEN, 128), f32),
    one128=((128, HEADS * 128), bf16),
    one64=((128, INNER), bf16),
    sum64=((INNER, 128), bf16),
    wdt=((MODEL, 128), bf16),
    acc=((10, 8, CONV_CH), f32),
)


def layer_kernel(x_ref, cot_ref, seg_ref, win, wout, sm, hd, mixed_ref, gtok_ref, dwin_ref, dwout_ref, gsm_ref, *refs):
    s = dict(zip(SCRATCH, refs))
    s["y"] = gtok_ref
    setup(seg_ref, win, s)
    chunks = LEN // CHUNK

    @pl.loop(0, SEQ)
    def _(q):
        project(q, x_ref, seg_ref, win, sm, hd, s)
        s["state"][...] = jnp.zeros((STATE, INNER), f32)

        @pl.loop(0, chunks)
        def _(c):
            scan_forward(q, c, seg_ref, sm, hd, s)

        @pl.loop(0, LEN // 256)
        def _(i):
            gate(q, i, x_ref, cot_ref, win, wout, sm, mixed_ref, s)

    for j in range(QUADS):
        cols = slice(j * 256, (j + 1) * 256)
        dwout_ref[cols, :] = tn(s["gated"][:, cols], cot_ref[...]).astype(bf16)

    @pl.loop(0, SEQ)
    def _(q):
        s["state"][...] = jnp.zeros((STATE, INNER), f32)

        @pl.loop(0, chunks)
        def _(c):
            scan_backward(q, chunks - 1 - c, seg_ref, sm, hd, s)

        conv_backward(q, sm, s)

    turned = s["gated"]
    for i in range(TOKENS // 128):
        for j in range(MODEL // 128):
            turned[j * 128 : (j + 1) * 128, i * 128 : (i + 1) * 128] = s["nrm"][
                i * 128 : (i + 1) * 128, j * 128 : (j + 1) * 128
            ].T
    for j in range(13):
        cols = slice(j * 256, (j + 1) * 256)
        of = s["dz"][:, cols] if j < QUADS else s["u"][:, j * 256 - INNER : (j + 1) * 256 - INNER]
        for i in range(3):
            rows = slice(i * 256, (i + 1) * 256)
            dwin_ref[rows, cols] = nn(turned[rows, :TOKENS], of).astype(bf16)
    dwin_ref[:, 3328:] = nn(turned[:MODEL, :TOKENS], s["ddt"][...]).astype(bf16)[:, :HEADS]

    @pl.loop(0, TOKENS // 256)
    def _(i):
        rows = pl.ds(pl.multiple_of(i * 256, 256), 256)
        for j in range(3):
            cols = slice(j * 256, (j + 1) * 256)
            gtok_ref[rows, cols] = (
                nt(s["dz"][rows, :], win[cols, :INNER])
                + nt(s["u"][rows, :], win[cols, INNER : INNER + CONV_CH])
                + nt(s["ddt"][rows, :], s["wdt"][cols, :])
            )

    @pl.loop(0, TOKENS // 128)
    def _(i):
        input_gradient(i, x_ref, cot_ref, sm, gtok_ref, s)

    for k in range(10):
        gsm_ref[k : k + 1, :] = jnp.sum(s["acc"][k], axis=0, keepdims=True)


def layer(x, cot, seg, win, wout, sm, hd):
    vmem = pl.BlockSpec(memory_space=pltpu.VMEM)
    return pl.pallas_call(
        layer_kernel,
        out_shape=(
            jax.ShapeDtypeStruct((TOKENS, MODEL), bf16),
            jax.ShapeDtypeStruct((TOKENS, MODEL), f32),
            jax.ShapeDtypeStruct((MODEL, PROJ), bf16),
            jax.ShapeDtypeStruct((INNER, MODEL), bf16),
            jax.ShapeDtypeStruct((10, CONV_CH), f32),
        ),
        in_specs=[vmem] * 7,
        out_specs=[vmem] * 5,
        scratch_shapes=[pltpu.VMEM(shape, kind) for shape, kind in SCRATCH.values()],
        compiler_params=pltpu.CompilerParams(vmem_limit_bytes=67043328),
        name="layer",
    )(x, cot, seg, win, wout, sm, hd)


def rows_to_lanes(v, width):
    return jnp.pad(v.astype(f32), (0, width - v.shape[0]))[None]


def on_device(tokens, segment_ids, norm_gain, in_weight, conv_weight, conv_bias, dt_bias, a_log, d_skip, gate_gain, out_weight, cotangent):
    win = lax.all_gather(in_weight, "shard", axis=0, tiled=True)
    wout = lax.all_gather(out_weight, "shard", axis=0, tiled=True)
    taps, bias, gain, first = lax.all_gather((conv_weight, conv_bias, gate_gain, norm_gain), "shard", axis=0, tiled=True)
    sm = jnp.concatenate(
        [
            taps.T.astype(f32),
            rows_to_lanes(bias, CONV_CH),
            rows_to_lanes(gain, CONV_CH),
            rows_to_lanes(first, CONV_CH),
            rows_to_lanes(jnp.repeat(d_skip, HEADDIM), CONV_CH),
        ],
        axis=0,
    )
    hd = jnp.concatenate([rows_to_lanes(dt_bias, 128), rows_to_lanes(a_log, 128), jnp.zeros((6, 128), f32)], axis=0)
    mixed, gtok, dwin, dwout, gsm = layer(
        tokens.reshape(TOKENS, MODEL), cotangent.reshape(TOKENS, MODEL), segment_ids, win, wout, sm, hd
    )
    dwin = lax.psum(lax.psum_scatter(dwin, "shard", scatter_dimension=0, tiled=True), "rep")
    dwout = lax.psum(lax.psum_scatter(dwout, "shard", scatter_dimension=0, tiled=True), "rep")
    gsm = lax.psum(gsm, ("rep", "shard"))
    me = lax.axis_index("shard")

    def owned(v, like):
        return lax.dynamic_slice_in_dim(v, me * like.shape[0], like.shape[0])

    return (
        mixed.reshape(SEQ, LEN, MODEL),
        gtok.reshape(SEQ, LEN, MODEL),
        owned(gsm[6, :MODEL], norm_gain),
        dwin.astype(f32),
        owned(gsm[:CONV].T, conv_weight),
        owned(gsm[4], conv_bias),
        gsm[8, :HEADS],
        gsm[9, :HEADS],
        gsm[7, :INNER].reshape(HEADS, HEADDIM).sum(axis=1),
        owned(gsm[5, :INNER], gate_gain),
        dwout.astype(f32),
    )


def solution(mesh):
    batch = P(("rep", "shard"), None, None)
    return jax.shard_map(
        on_device,
        mesh=mesh,
        in_specs=(
            batch,
            P(("rep", "shard"), None),
            P("shard"),
            P("shard", None),
            P("shard", None),
            P("shard"),
            P(),
            P(),
            P(),
            P("shard"),
            P("shard", None),
            batch,
        ),
        out_specs=(
            batch,
            batch,
            P("shard"),
            P("shard", None),
            P("shard", None),
            P("shard"),
            P(),
            P(),
            P(),
            P("shard"),
            P("shard", None),
        ),
        check_vma=False,
    )
```

profile of v0, /device:TPU:0, one launch (start us, length us, event | category | flops | bytes accessed | tf_op | source)
XLA Modules:
  0.0 619.1 jit_solution(6311611740049517533)
XLA Ops:
  7.2 0.0 copy-start.8
  7.2 0.0 copy-start.2
  7.2 0.0 copy-start.7
  7.2 0.0 copy-start.1
  7.2 0.0 copy-start.4
  7.2 0.0 copy-start.3
  7.2 0.0 copy-start.6
  7.3 0.0 copy-start.5
  7.3 0.0 all-gather.7.cloned.1.call-start
  7.3 0.7 all-gather.7.cloned.1.call-update
  8.0 0.0 all-gather.5.cloned.1.call-start
  8.0 0.7 all-gather.5.cloned.1.call-update
  8.7 0.0 reduce-scatter.5.cloned.1.call-start
  8.8 0.0 copy-done.8
  8.8 0.6 dynamic-slice.7
  10.7 0.0 copy-done.2
  10.7 0.3 dynamic-update-slice
  11.0 0.0 copy-done.7
  11.0 0.2 dynamic-update-slice.1
  11.2 13.8 %all-reduce.8 = (bf16[1792]{0:T(1024)(128)(2,1)S(1)}, bf16[768]{0:T(1024)(128)(2,1)S(1)}) all-reduce(bf16[1792]{0:T(1024)(128)(2,1)S(1)} %dynamic-update-slice, bf16[768]{0:T(1024)(128)(2,1)S(1)} %dynamic-update-slice.1), channel_id=1, replica_groups=mesh['rep'=8,'shard'=4] {'shard'}, use_global_device_ids=true, to_apply=%add.5 | all-reduce | flops 2560 | bytes 10240
  25.1 0.0 copy-done.1
  25.1 13.9 %all-gather = bf16[4,448,4]{1,2,0:T(4,128)(2,1)S(1)} all-gather(bf16[1,448,4]{1,2,0:T(4,128)(2,1)S(1)} %bitcast.25), channel_id=1, replica_groups=mesh['rep'=8,'shard'=4] {'shard'}, dimensions={0}, use_global_device_ids=true | all-gather | bytes 17920 | tf_op jit(solution)/shard_map/all_gather | solution.py:502
  39.0 0.1 reshape.58
  39.1 0.0 copy-done.4
  39.1 0.1 broadcast_in_dim.39
  39.1 0.1 reshape.42
  39.2 0.0 copy-done.3
  39.3 12.4 %all-gather.1 = bf16[4,1,384]{2,1,0:T(2,128)(2,1)S(1)} all-gather(bf16[1,1,384]{2,1,0:T(2,128)(2,1)S(1)} %reshape.56), channel_id=1, replica_groups=mesh['rep'=8,'shard'=4] {'shard'}, dimensions={0}, use_global_device_ids=true | all-gather | bytes 3840 | tf_op jit(solution)/shard_map/all_gather | solution.py:502
  51.8 0.1 pad.27.clone
  51.8 0.7 concatenate.6.sm
  52.5 0.0 copy-done.6
  52.5 0.0 copy-done.5
  52.5 0.7 maximum_maximum_fusion.hd
  53.2 10.0 %all-gather.7.cloned.1.call-done.wout = bf16[1536,768]{1,0:T(8,128)(2,1)} async-done(((bf16[384,768]{1,0:T(8,128)(2,1)}), bf16[1536,768]{1,0:T(8,128)(2,1)}) %all-gather.7.cloned.1.call-update) | async-done | bytes 2359312 | tf_op jit(solution)/shard_map/all_gather | solution.py:501
  63.2 99.5 %all-gather.5.cloned.1.call-done.win = bf16[768,3352]{1,0:T(8,128)(2,1)} async-done(((bf16[192,3352]{1,0:T(8,128)(2,1)}), bf16[768,3352]{1,0:T(8,128)(2,1)}) %all-gather.5.cloned.1.call-update) | async-done | bytes 5148688 | tf_op jit(solution)/shard_map/all_gather | solution.py:500
  162.7 108.6 %layer.1 = (bf16[1024,768]{1,0:T(8,128)(2,1)}, f32[1024,768]{1,0:T(8,128)}, bf16[768,3352]{1,0:T(8,128)(2,1)}, bf16[1536,768]{1,0:T(8,128)(2,1)}, f32[10,1792]{1,0:T(8,128)}) custom-call(bf16[1024,768]{1,0:T(8,128)(2,1)} %bitcast.22, bf16[1024,768]{1,0:T(8,128)(2,1)} %bitcast.23, s32[2,512]{1,0:T(2,128)} %seg_ref.1, ...), custom_call_target="tpu_custom_call" | custom-call | tf_op jit(solution)/shard_map/layer/pallas_call | solution.py:478
  271.3 0.0 reduce-scatter.5.cloned.1.call-update
  271.3 0.0 reduce-scatter.3.cloned.1.call-start
  271.3 0.5 reduce-scatter.3.cloned.1.call-update
  271.9 0.0 all-reduce.12.cloned.1.call-start
  271.9 0.5 all-reduce.12.cloned.1.call-update
  272.4 0.0 all-reduce.14.cloned.1.call-start
  272.5 45.0 %reduce-scatter.5.cloned.1.call-done = bf16[384,768]{1,0:T(8,128)(2,1)} async-done(((bf16[1536,768]{1,0:T(8,128)(2,1)}), bf16[384,768]{1,0:T(8,128)(2,1)}) %reduce-scatter.5.cloned.1.call-update) | async-done | bytes 589840 | tf_op jit(solution)/shard_map/reduce_scatter | solution.py:518
  317.5 96.4 %reduce-scatter.3.cloned.1.call-done = bf16[192,3352]{1,0:T(8,128)(2,1)} async-done(((bf16[768,3352]{1,0:T(8,128)(2,1)}), bf16[192,3352]{1,0:T(8,128)(2,1)}) %reduce-scatter.3.cloned.1.call-update) | async-done | bytes 1287184 | tf_op jit(solution)/shard_map/reduce_scatter | solution.py:517
  413.9 0.0 all-reduce.14.cloned.1.call-update
  413.9 129.1 %all-reduce.12.cloned.1.call-done = f32[10,1792]{1,0:T(8,128)} async-done(((f32[10,1792]{1,0:T(8,128)}), f32[10,1792]{1,0:T(8,128)}) %all-reduce.12.cloned.1.call-update) | async-done | bytes 71696 | tf_op jit(solution)/shard_map/psum | solution.py:519
  543.1 0.9 fusion
  544.0 0.1 reshape_squeeze.3
  544.0 0.6 reduce_sum.9
  544.7 0.8 slice.29
  545.5 0.8 slice.30
  546.3 0.7 slice.28
  547.1 0.6 dynamic-slice_reduce_fusion
  547.7 0.6 constant_dynamic-slice_fusion.1
  548.3 0.7 constant_dynamic-slice_fusion
  548.9 0.7 dynamic-slice_bitcast_fusion
  549.6 1.3 slice_bitcast_fusion
  550.9 57.3 %all-reduce.14.cloned.1.call-done = (bf16[192,3352]{1,0:T(8,128)(2,1)}, bf16[384,768]{1,0:T(8,128)(2,1)}) async-done(((bf16[192,3352]{1,0:T(8,128)(2,1)}, bf16[384,768]{1,0:T(8,128)(2,1)}), (bf16[192,3352]{1,0:T(8,128)(2,1)}, bf16[384,768]{1,0:T(8,128)(2,1)})) %all-reduce.14.cloned.1.call-update) | async-done | bytes 1877008 | tf_op jit(solution)/shard_map/psum | solution.py:517
  608.1 0.0 copy-start
  608.1 3.1 convert_element_type.25
  611.2 0.0 copy-done
  611.2 1.1 convert_element_type.26
  (15 shorter events, 0.1 us)
Async XLA Ops:
  7.2 1.6 copy-start.8
  7.2 3.5 copy-start.2
  7.2 3.8 copy-start.7
  7.2 17.9 %copy-start.1 = (bf16[448,4]{0,1:T(4,128)(2,1)S(1)}, bf16[448,4]{0,1:T(4,128)(2,1)}, u32[]{:S(2)}) copy-start(bf16[448,4]{0,1:T(4,128)(2,1)} %param.16) | copy-start | bytes 10756
  7.2 31.8 %copy-start.4 = (f32[24]{0:T(128)S(1)}, f32[24]{0:T(128)}, u32[]{:S(2)}) copy-start(f32[24]{0:T(128)} %param.20) | copy-start | bytes 292
  7.2 32.0 %copy-start.3 = (bf16[384]{0:T(512)(128)(2,1)S(1)}, bf16[384]{0:T(512)(128)(2,1)}, u32[]{:S(2)}) copy-start(bf16[384]{0:T(512)(128)(2,1)} %param.21) | copy-start | bytes 2308
  7.2 45.3 %copy-start.6 = (f32[24]{0:T(128)S(1)}, f32[24]{0:T(128)}, u32[]{:S(2)}) copy-start(f32[24]{0:T(128)} %param.18) | copy-start | bytes 292
  7.3 45.3 %copy-start.5 = (f32[24]{0:T(128)S(1)}, f32[24]{0:T(128)}, u32[]{:S(2)}) copy-start(f32[24]{0:T(128)} %param.19) | copy-start | bytes 292
  7.3 55.9 %all-gather.7.cloned.1.call-start = ((), (), s32[]{:S(2)}) async-start(), calls=%async_computation.3 | async-start | bytes 2949120 | tf_op jit(solution)/shard_map/all_gather | solution.py:501
  8.0 154.7 %all-gather.5.cloned.1.call-start = ((), (), s32[]{:S(2)}) async-start(), calls=%async_computation.2 | async-start | bytes 6635520 | tf_op jit(solution)/shard_map/all_gather | solution.py:500
  8.7 308.7 %reduce-scatter.5.cloned.1.call-start = ((), (), s32[]{:S(2)}) async-start(), calls=%async_computation.6 | async-start | bytes 2949120 | tf_op jit(solution)/shard_map/reduce_scatter | solution.py:518
  271.3 142.6 %reduce-scatter.3.cloned.1.call-start = ((), (), s32[]{:S(2)}) async-start(), calls=%async_computation.5 | async-start | bytes 6635520 | tf_op jit(solution)/shard_map/reduce_scatter | solution.py:517
  271.9 271.2 %all-reduce.12.cloned.1.call-start = ((), (), s32[]{:S(2)}) async-start(), calls=%async_computation.4 | async-start | bytes 229376 | tf_op jit(solution)/shard_map/psum | solution.py:519
  272.4 335.7 %all-reduce.14.cloned.1.call-start = ((), (), s32[]{:S(2)}) async-start(), calls=%async_computation.7 | async-start | bytes 3833856 | tf_op jit(solution)/shard_map/psum | solution.py:517
  608.1 3.1 copy-start
Sparse Core Ops, SparseCore 0:
  9.6 53.4 all-gather.6
  64.7 97.9 all-gather.4
  271.4 46.0 reduce-scatter.4
  319.6 94.2 reduce-scatter.2
  419.9 123.1 all-reduce.11
  546.4 61.7 all-reduce.13
where the time goes:
time: 620 us; the launch traced here: 619 us
  waiting for transfers between devices  440 us (71%)
  Pallas kernels  109 us (18%)
  blocking collectives  40.1 us (6%)
  between operations  15.6 us (3%)
  local copies, waits for them, and re-layouts  9.35 us (2%)
    psum x1, waiting for transfers between devices, on_device(): gsm = lax.psum(gsm, ('rep', 'shard'))  129 us
    pallas_call x1, Pallas kernels, layer(): pl.pallas_call(layer_kernel, out_shape=(jax.ShapeDtypeStruct((TOKENS, MOD...  109 us
    all_gather x1, waiting for transfers between devices, on_device(): win = lax.all_gather(in_weight, 'shard', axis=0, tiled=True)  99.5 us
    reduce_scatter x1, waiting for transfers between devices, on_device(): lax.psum_scatter(dwin, 'shard', scatter_dimension=0, tiled=True)  96.4 us
    psum x1, waiting for transfers between devices, on_device(): lax.psum(lax.psum_scatter(dwin, 'shard', scatter_dimension=0, tiled=True)...  57.3 us
    reduce_scatter x1, waiting for transfers between devices, on_device(): lax.psum_scatter(dwout, 'shard', scatter_dimension=0, tiled=True)  45 us
    all_gather x2, blocking collectives, on_device(): lax.all_gather((conv_weight, conv_bias, gate_gain, norm_gain), 'shard', a...  26.3 us
    unnamed x1, blocking collectives  13.8 us
  transfers between devices with their start and end apart: 6, of which 6 were waited for; matrix products, arithmetic and copies ran while one was open for 2% of the time, Pallas kernels for 0%

commit v1 on v0

--- a/solution.py
+++ b/solution.py
@@ -15,8 +15,10 @@
 CONV_CH = 1792
 MODEL = 768
 PROJ = 3352
-PADDED = 3456
+PADDED = 3584
+DT = INNER + CONV_CH
 EPS = 1e-05
+MESH = pl.DeviceIdType.MESH
 
 LEN = 512
 CHUNK = 128
@@ -82,7 +84,113 @@
     return pl.ds(pl.multiple_of(base + row, 8), count), slice(cols.start - shift, cols.stop - shift)
 
 
-def setup(seg_ref, win, s):
+def place():
+    rep, shard = lax.axis_index("rep"), lax.axis_index("shard")
+    core = rep % 2
+    px, py = (rep // 2) % 2, rep // 4
+    a = px * (1 - core) + py * core
+    b = py * (1 - core) + px * core
+    return dict(
+        rep=rep,
+        shard=shard,
+        core=core,
+        a=a,
+        b=b,
+        one=rep + (1 - 2 * a) * (2 + 2 * core),
+        two=rep + (1 - 2 * b) * (4 - 2 * core),
+        mate=rep + 1 - 2 * core,
+    )
+
+
+def greet(at, shards):
+    barrier = pltpu.get_barrier_semaphore()
+    for who in ("one", "two", "mate"):
+        pl.semaphore_signal(barrier, inc=1, device_id=(at[who], at["shard"]), device_id_type=MESH)
+    for d in range(1, shards):
+        pl.semaphore_signal(
+            barrier, inc=1, device_id=(at["rep"], (at["shard"] + d) % shards), device_id_type=MESH
+        )
+    pl.semaphore_wait(barrier, 2 + shards)
+
+
+def remote(src, dst, send, recv, rep, shard):
+    return pltpu.make_async_remote_copy(
+        src_ref=src, dst_ref=dst, send_sem=send, recv_sem=recv, device_id=(rep, shard), device_id_type=MESH
+    )
+
+
+class Gather:
+    def __init__(self, at, ref, shards, rows, start, half, sems, part):
+        self.at, self.ref, self.shards, self.rows, self.start, self.half = at, ref, shards, rows, start, half
+        self.send, self.recv = (lambda kind, d: sems[0].at[part, kind, d]), (lambda kind, d: sems[1].at[part, kind, d])
+
+    def columns(self):
+        return pl.ds(pl.multiple_of(self.start + self.at["core"] * self.half, 128), self.half)
+
+    def piece(self, shard, a, b):
+        tall = self.rows // 4
+        return self.ref.at[pl.ds(pl.multiple_of(shard * self.rows + (2 * b + a) * tall, 16), tall), self.columns()]
+
+    def strip(self, shard):
+        return self.ref.at[pl.ds(pl.multiple_of(shard * self.rows, 16), self.rows), self.columns()]
+
+    def source(self, d):
+        return (self.at["shard"] + self.shards - d) % self.shards
+
+    def copy(self, kind, d):
+        at = self.at
+        if kind == 0:
+            own = self.piece(at["shard"], at["a"], at["b"])
+            return remote(own, own, self.send(0, d), self.recv(0, d), at["rep"], (at["shard"] + d) % self.shards)
+        if kind == 4:
+            what, who = self.strip(self.source(d)), at["mate"]
+        elif kind == 3:
+            what, who = self.piece(self.source(d), at["a"], 1 - at["b"]), at["one"]
+        else:
+            what, who = self.piece(self.source(d), at["a"], at["b"]), at["one"] if kind == 1 else at["two"]
+        return remote(what, what, self.send(kind, d), self.recv(kind, d), who, at["shard"])
+
+    def each(self):
+        return range(1, self.shards)
+
+    def begin(self):
+        for d in self.each():
+            self.copy(0, d).start()
+
+    def spread(self):
+        for d in self.each():
+            self.copy(0, d).wait_recv()
+            self.copy(2, d).start()
+            self.copy(1, d).start()
+
+    def relay(self):
+        for d in self.each():
+            self.copy(2, d).wait_recv()
+            self.copy(3, d).start()
+
+    def share(self):
+        for d in self.each():
+            self.copy(1, d).wait_recv()
+            self.copy(3, d).wait_recv()
+            self.copy(4, d).start()
+
+    def finish(self):
+        for d in self.each():
+            self.copy(4, d).wait_recv()
+            for kind in range(5):
+                self.copy(kind, d).wait_send()
+
+
+def spread_lanes(block, width, offset):
+    total = jnp.zeros((8, CONV_CH), f32)
+    for z in range(4):
+        part = jnp.where(lanes_of((8, 512)) < width, block[z], 0.0)
+        part = jnp.concatenate([part, jnp.zeros((8, CONV_CH - 512), f32)], axis=1)
+        total = total + (part if z == 0 else pltpu.roll(part, z * offset, 1))
+    return total
+
+
+def setup(seg_ref, s):
     r, c = rows_of((128, 256)), lanes_of((128, 256))
     for j in range(HEADS * 128 // 256):
         s["one128"][:, j * 256 : (j + 1) * 256] = (
@@ -95,8 +203,6 @@
     r, c = rows_of((256, 128)), lanes_of((256, 128))
     for j in range(QUADS):
         s["sum64"][j * 256 : (j + 1) * 256, :] = (((r + j * 256) >> 6) == c).astype(f32).astype(bf16)
-    s["wdt"][...] = jnp.zeros((MODEL, 128), bf16)
-    s["wdt"][:, :HEADS] = win[:, INNER + CONV_CH : PROJ]
     s["acc"][...] = jnp.zeros(s["acc"].shape, f32)
     s["pre"][TOKENS:, :] = jnp.zeros((16, CONV_CH), bf16)
     s["up"][:, 0:8, :] = jnp.zeros((2, 8, 256), f32)
@@ -119,7 +225,7 @@
     for o in range(1, CONV):
         s["back"][o - 1] = ((seg == pltpu.roll(seg, o, 0)) & (place >= o)).astype(f32)
     rows = pl.ds(row0, LEN)
-    raw = nn(s["nrm"][rows, :], s["wdt"][...]) + hd[0:1, :]
+    raw = nn(s["nrm"][rows, :], win[:, DT : DT + 128]) + hd[0:1, :128]
     s["dtx"][rows, :] = raw
     for j in range(CONV_CH // 256):
         slot = j % 2
@@ -145,7 +251,7 @@
     rows = pl.ds(row0, CHUNK)
     raw = s["dtx"][rows, :]
     dt = jnp.maximum(raw, 0.0) + jnp.log1p(jnp.exp(-jnp.abs(raw)))
-    rate = -jnp.exp(hd[1:2, :]) * dt
+    rate = -jnp.exp(hd[1:2, :128]) * dt
     lower = (rows_of((CHUNK, CHUNK)) >= lanes_of((CHUNK, CHUNK))).astype(f32)
     cum = exact(lower, rate)
     source = cum - jnp.log(jnp.maximum(dt, 1e-37))
@@ -256,7 +362,10 @@
     high, low = two_parts(s["dg"][...])
     s["rowdot"][rows, :] = nn(high, s["sum64"][...]) + nn(low, s["sum64"][...])
     branch = nn(s["gated"][rows, :], wout[...])
-    mixed_ref[rows, :] = (x_ref[rows, :].astype(f32) + branch).astype(bf16)
+    s["mixed"][...] = (x_ref[rows, :].astype(f32) + branch).astype(bf16)
+    out = pltpu.make_async_copy(s["mixed"], mixed_ref.at[rows, :], s["mixed_sem"])
+    out.start()
+    out.wait()
 
 
 def scan_backward(q, c, seg_ref, sm, hd, s):
@@ -330,7 +439,7 @@
     drate = exact(allowed.astype(f32), dcum) + dlast * (segc == segc[CHUNK - 1 : CHUNK]).astype(f32)
     sg = sigmoid(raw)
     ratio = jnp.where(dt > 1e-30, sg / jnp.maximum(dt, 1e-30), 1.0)
-    draw = colsum * ratio - drate * jnp.exp(hd[1:2, :]) * sg
+    draw = colsum * ratio - drate * jnp.exp(hd[1:2, :128]) * sg
     draw = jnp.where(lanes_of((CHUNK, 128)) < HEADS, draw, 0.0)
     s["ddt"][rows, :] = draw.astype(bf16)
     s["acc"][8, :, 0:128] += partial_sum(draw)
@@ -376,6 +485,11 @@
 
 
 SCRATCH = dict(
+    win=((MODEL, PADDED), bf16),
+    wout=((INNER, MODEL), bf16),
+    parts=((4, 8, 512), f32),
+    sm=((8, CONV_CH), f32),
+    mixed=((256, MODEL), bf16),
     nrm=((TOKENS, MODEL), bf16),
     u=((TOKENS, CONV_CH), bf16),
     pre=((TOKENS + 16, CONV_CH), bf16),
@@ -402,15 +516,100 @@
     one128=((128, HEADS * 128), bf16),
     one64=((128, INNER), bf16),
     sum64=((INNER, 128), bf16),
-    wdt=((MODEL, 128), bf16),
     acc=((10, 8, CONV_CH), f32),
 )
 
 
-def layer_kernel(x_ref, cot_ref, seg_ref, win, wout, sm, hd, mixed_ref, gtok_ref, dwin_ref, dwout_ref, gsm_ref, *refs):
+def gather_weights(shards, seg_ref, win_own, wout_own, sm_own, hd, s, send_sems, recv_sems, small_send, small_recv):
+    win, wout, sm = s["win"], s["wout"], s["sm"]
+    at = place()
+    shard = at["shard"]
+    rows = pl.ds(pl.multiple_of(shard * (MODEL // shards), 16), MODEL // shards)
+    win[rows, DT:] = jnp.zeros((MODEL // shards, PADDED - DT), bf16)
+    win[rows, :PROJ] = win_own[...]
+    wout[pl.ds(pl.multiple_of(shard * (INNER // shards), 16), INNER // shards), :] = wout_own[...]
+    s["parts"][shard] = sm_own[...]
+    greet(at, shards)
+    sems = (send_sems, recv_sems)
+    conv_part = Gather(at, win, shards, MODEL // shards, INNER, (PADDED - INNER) // 2, sems, 0)
+    gate_part = Gather(at, win, shards, MODEL // shards, 0, INNER // 2, sems, 1)
+    out_part = Gather(at, wout, shards, INNER // shards, 0, MODEL // 2, sems, 2)
+
+    def small(d):
+        return remote(
+            s["parts"].at[shard],
+            s["parts"].at[shard],
+            small_send.at[d],
+            small_recv.at[d],
+            at["rep"],
+            (shard + d) % shards,
+        )
+
+    for d in range(1, shards):
+        small(d).start()
+    conv_part.begin()
+    setup(seg_ref, s)
+    conv_part.spread()
+    gate_part.begin()
+    out_part.begin()
+    conv_part.relay()
+    conv_part.share()
+    for d in range(1, shards):
+        small(d).wait_recv()
+        small(d).wait_send()
+    row = rows_of((8, CONV_CH))
+    taps = spread_lanes(s["parts"], 448, 448)
+    gain = spread_lanes(s["parts"], 384, 384)
+    first = spread_lanes(s["parts"], 192, 192)
+    sm[...] = jnp.where(row < 5, taps, jnp.where(row == 5, gain, first))
+    sm[7:8, :] = hd[2:3, :]
+    conv_part.finish()
+    for part in (gate_part, out_part):
+        part.spread()
+        part.relay()
+        part.share()
+    for part in (gate_part, out_part):
+        part.finish()
+
+
+def copy_weights(seg_ref, win_all, wout_all, sm_all, hd, s, sems):
+    copies = [
+        pltpu.make_async_copy(src, s[name], sems.at[i])
+        for i, (src, name) in enumerate(((win_all, "win"), (wout_all, "wout"), (sm_all, "sm")))
+    ]
+    for copy in copies:
+        copy.start()
+    setup(seg_ref, s)
+    for copy in copies:
+        copy.wait()
+    s["sm"][7:8, :] = hd[2:3, :]
+
+
+def layer_kernel(
+    direct,
+    shards,
+    x_ref,
+    cot_ref,
+    seg_ref,
+    win_own,
+    wout_own,
+    sm_own,
+    hd,
+    mixed_ref,
+    gtok_ref,
+    dwin_ref,
+    dwout_ref,
+    gsm_ref,
+    *refs,
+):
     s = dict(zip(SCRATCH, refs))
+    s["mixed_sem"], *sems = refs[len(SCRATCH) :]
     s["y"] = gtok_ref
-    setup(seg_ref, win, s)
+    win, wout, sm = s["win"], s["wout"], s["sm"]
+    if direct:
+        gather_weights(shards, seg_ref, win_own, wout_own, sm_own, hd, s, *sems)
+    else:
+        copy_weights(seg_ref, win_own, wout_own, sm_own, hd, s, *sems)
     chunks = LEN // CHUNK
 
     @pl.loop(0, SEQ)
@@ -462,7 +661,7 @@
             gtok_ref[rows, cols] = (
                 nt(s["dz"][rows, :], win[cols, :INNER])
                 + nt(s["u"][rows, :], win[cols, INNER : INNER + CONV_CH])
-                + nt(s["ddt"][rows, :], s["wdt"][cols, :])
+                + nt(s["ddt"][rows, :], win[cols, DT : DT + 128])
             )
 
     @pl.loop(0, TOKENS // 128)
@@ -473,10 +672,23 @@
         gsm_ref[k : k + 1, :] = jnp.sum(s["acc"][k], axis=0, keepdims=True)
 
 
-def layer(x, cot, seg, win, wout, sm, hd):
+def reaches(mesh):
+    return mesh.shape["rep"] == 8 and mesh.shape["shard"] == 4
+
+
+def layer(mesh, x, cot, seg, win, wout, sm, hd):
+    direct, shards = reaches(mesh), mesh.shape["shard"]
     vmem = pl.BlockSpec(memory_space=pltpu.VMEM)
+    hbm = pl.BlockSpec(memory_space=pl.ANY)
+    dma = pltpu.SemaphoreType.DMA
+    if direct:
+        sems = [dma((3, 5, shards)), dma((3, 5, shards)), dma((shards,)), dma((shards,))]
+        options = dict(collective_id=0, has_side_effects=True)
+        weights = vmem
+    else:
+        sems, options, weights = [dma((3,))], {}, hbm
     return pl.pallas_call(
-        layer_kernel,
+        partial(layer_kernel, direct, shards),
         out_shape=(
             jax.ShapeDtypeStruct((TOKENS, MODEL), bf16),
             jax.ShapeDtypeStruct((TOKENS, MODEL), f32),
@@ -484,10 +696,10 @@
             jax.ShapeDtypeStruct((INNER, MODEL), bf16),
             jax.ShapeDtypeStruct((10, CONV_CH), f32),
         ),
-        in_specs=[vmem] * 7,
-        out_specs=[vmem] * 5,
-        scratch_shapes=[pltpu.VMEM(shape, kind) for shape, kind in SCRATCH.values()],
-        compiler_params=pltpu.CompilerParams(vmem_limit_bytes=67043328),
+        in_specs=[vmem] * 3 + [weights] * 3 + [vmem],
+        out_specs=[hbm] + [vmem] * 4,
+        scratch_shapes=[pltpu.VMEM(shape, kind) for shape, kind in SCRATCH.values()] + [dma] + sems,
+        compiler_params=pltpu.CompilerParams(vmem_limit_bytes=67043328, **options),
         name="layer",
     )(x, cot, seg, win, wout, sm, hd)
 
@@ -496,22 +708,24 @@
     return jnp.pad(v.astype(f32), (0, width - v.shape[0]))[None]
 
 
-def on_device(tokens, segment_ids, norm_gain, in_weight, conv_weight, conv_bias, dt_bias, a_log, d_skip, gate_gain, out_weight, cotangent):
-    win = lax.all_gather(in_weight, "shard", axis=0, tiled=True)
-    wout = lax.all_gather(out_weight, "shard", axis=0, tiled=True)
-    taps, bias, gain, first = lax.all_gather((conv_weight, conv_bias, gate_gain, norm_gain), "shard", axis=0, tiled=True)
-    sm = jnp.concatenate(
-        [
-            taps.T.astype(f32),
-            rows_to_lanes(bias, CONV_CH),
-            rows_to_lanes(gain, CONV_CH),
-            rows_to_lanes(first, CONV_CH),
-            rows_to_lanes(jnp.repeat(d_skip, HEADDIM), CONV_CH),
-        ],
+def on_device(mesh, tokens, segment_ids, norm_gain, in_weight, conv_weight, conv_bias, dt_bias, a_log, d_skip, gate_gain, out_weight, cotangent):
+    small = (conv_bias, gate_gain, norm_gain)
+    if reaches(mesh):
+        win, wout = in_weight, out_weight
+        sm = jnp.concatenate([conv_weight.T.astype(f32)] + [rows_to_lanes(v, 512 - 64) for v in small + (norm_gain,)])
+        sm = jnp.pad(sm, ((0, 0), (0, 64)))
+    else:
+        win, wout, taps, *small = lax.all_gather(
+            (in_weight, out_weight, conv_weight) + small, "shard", axis=0, tiled=True
+        )
+        win = jnp.pad(win, ((0, 0), (0, PADDED - PROJ)))
+        sm = jnp.concatenate([taps.T.astype(f32)] + [rows_to_lanes(v, CONV_CH) for v in (*small, small[-1])])
+    hd = jnp.concatenate(
+        [rows_to_lanes(v, CONV_CH) for v in (dt_bias, a_log, jnp.repeat(d_skip, HEADDIM))] + [jnp.zeros((5, CONV_CH), f32)],
         axis=0,
     )
-    hd = jnp.concatenate([rows_to_lanes(dt_bias, 128), rows_to_lanes(a_log, 128), jnp.zeros((6, 128), f32)], axis=0)
     mixed, gtok, dwin, dwout, gsm = layer(
+        mesh,
         tokens.reshape(TOKENS, MODEL), cotangent.reshape(TOKENS, MODEL), segment_ids, win, wout, sm, hd
     )
     dwin = lax.psum(lax.psum_scatter(dwin, "shard", scatter_dimension=0, tiled=True), "rep")
@@ -540,7 +754,7 @@
 def solution(mesh):
     batch = P(("rep", "shard"), None, None)
     return jax.shard_map(
-        on_device,
+        partial(on_device, mesh),
         mesh=mesh,
         in_specs=(
             batch,

time: 620 us -> 483 us (0.78)
  waiting for transfers between devices: 440 us -> 285 us
  Pallas kernels: 109 us -> 159 us
  blocking collectives: 40.1 us -> 0 us
  local copies, waits for them, and re-layouts: 9.35 us -> 17 us
    all_gather x2 -> x0, waiting for transfers between devices: 109 us -> none  [the longest x1 99.5 us: on_device(): win = lax.all_gather(in_weight, 'shard', axis=0, tiled=True)]
    pallas_call x1, Pallas kernels: 109 us -> 159 us  [layer(): pl.pallas_call(partial(layer_kernel, direct, shards), out_shape=(jax.Shap...]
    psum x1, waiting for transfers between devices: 129 us -> 82.1 us  [on_device(): gsm = lax.psum(gsm, ('rep', 'shard'))]
    all_gather x2 -> x0, blocking collectives: 26.3 us -> none  [on_device(): lax.all_gather((conv_weight, conv_bias, gate_gain, norm_gain), 'shard', a...]
    unnamed x1 -> x0, blocking collectives: 13.8 us -> none
  transfers between devices with their start and end apart: 6 -> 4, of which waited for: 6 -> 4; matrix products, arithmetic and copies ran while one was open for 2% -> 2% of each run, Pallas kernels for 0% -> 0%
where the time goes in v1:
time: 483 us
  waiting for transfers between devices  285 us (59%)
  Pallas kernels  159 us (33%)
  local copies, waits for them, and re-layouts  17 us (4%)
  between operations  15.5 us (3%)
  other arithmetic  6.09 us (1%)
    pallas_call x1, Pallas kernels, layer(): pl.pallas_call(partial(layer_kernel, direct, shards), out_shape=(jax.Shap...  159 us
    reduce_scatter x1, waiting for transfers between devices, on_device(): lax.psum_scatter(dwin, 'shard', scatter_dimension=0, tiled=True)  96.8 us
    psum x1, waiting for transfers between devices, on_device(): gsm = lax.psum(gsm, ('rep', 'shard'))  82.1 us
    psum x1, waiting for transfers between devices, on_device(): lax.psum(lax.psum_scatter(dwin, 'shard', scatter_dimension=0, tiled=True)...  56.8 us
    reduce_scatter x1, waiting for transfers between devices, on_device(): lax.psum_scatter(dwout, 'shard', scatter_dimension=0, tiled=True)  47.8 us
  transfers between devices with their start and end apart: 4, of which 4 were waited for; matrix products, arithmetic and copies ran while one was open for 2% of the time, Pallas kernels for 0%

profile of v1, /device:TPU:0, one launch (start us, length us, event | category | flops | bytes accessed | tf_op | source)
XLA Modules:
  0.0 482.5 jit_solution(17085093934777898918)
XLA Ops:
  8.0 0.0 reduce-scatter.5.cloned.1.call-start
  8.1 0.7 broadcast_in_dim.33
  8.8 0.1 reshape.42
  8.9 0.7 pad.32
  9.5 0.7 pad.33
  10.2 0.7 pad.28
  10.9 0.7 pad.29
  11.6 0.7 broadcast_in_dim.28
  12.3 0.7 concatenate.7
  13.0 0.6 pad_convert_fusion.sm_own
  13.6 0.1 pad.38.clone
  13.7 0.7 maximum_maximum_fusion.hd
  14.4 158.9 %layer.1 = (bf16[1024,768]{1,0:T(8,128)(2,1)}, f32[1024,768]{1,0:T(8,128)}, bf16[768,3352]{1,0:T(8,128)(2,1)}, bf16[1536,768]{1,0:T(8,128)(2,1)}, f32[10,1792]{1,0:T(8,128)}) custom-call(bf16[1024,768]{1,0:T(8,128)(2,1)} %bitcast.15, bf16[1024,768]{1,0:T(8,128)(2,1)} %bitcast.16, s32[2,512]{1,0:T(2,128)} %seg_ref.1, bf16[192,3352]{1,0:T(8,128)(2,1)} %win_own.1, ...), custom_call_target="tpu_custom_call" | custom-call | tf_op jit(solution)/shard_map/layer/pallas_call | solution.py:690
  173.2 0.0 reduce-scatter.5.cloned.1.call-update
  173.3 0.0 reduce-scatter.3.cloned.1.call-start
  173.3 0.7 reduce-scatter.3.cloned.1.call-update
  174.0 0.0 all-reduce.10.cloned.1.call-start
  174.1 0.5 all-reduce.10.cloned.1.call-update
  174.6 0.0 all-reduce.12.cloned.1.call-start
  174.6 47.8 %reduce-scatter.5.cloned.1.call-done = bf16[384,768]{1,0:T(8,128)(2,1)} async-done(((bf16[1536,768]{1,0:T(8,128)(2,1)}), bf16[384,768]{1,0:T(8,128)(2,1)}) %reduce-scatter.5.cloned.1.call-update) | async-done | bytes 589840 | tf_op jit(solution)/shard_map/reduce_scatter | solution.py:732
  222.5 96.8 %reduce-scatter.3.cloned.1.call-done = bf16[192,3352]{1,0:T(8,128)(2,1)} async-done(((bf16[768,3352]{1,0:T(8,128)(2,1)}), bf16[192,3352]{1,0:T(8,128)(2,1)}) %reduce-scatter.3.cloned.1.call-update) | async-done | bytes 1287184 | tf_op jit(solution)/shard_map/reduce_scatter | solution.py:731
  319.3 0.0 all-reduce.12.cloned.1.call-update
  319.3 82.1 %all-reduce.10.cloned.1.call-done = f32[10,1792]{1,0:T(8,128)} async-done(((f32[10,1792]{1,0:T(8,128)}), f32[10,1792]{1,0:T(8,128)}) %all-reduce.10.cloned.1.call-update) | async-done | bytes 71696 | tf_op jit(solution)/shard_map/psum | solution.py:733
  401.4 0.9 fusion
  402.3 0.1 reshape_squeeze.3
  402.4 0.6 reduce_sum.9
  403.0 0.8 slice.29
  403.9 0.8 slice.30
  404.7 0.7 slice.28
  405.4 0.6 dynamic-slice_reduce_fusion
  406.0 0.6 constant_dynamic-slice_fusion.1
  406.7 0.7 constant_dynamic-slice_fusion
  407.3 0.7 dynamic-slice_bitcast_fusion
  408.0 1.3 slice_bitcast_fusion
  409.3 56.8 %all-reduce.12.cloned.1.call-done = (bf16[192,3352]{1,0:T(8,128)(2,1)}, bf16[384,768]{1,0:T(8,128)(2,1)}) async-done(((bf16[192,3352]{1,0:T(8,128)(2,1)}, bf16[384,768]{1,0:T(8,128)(2,1)}), (bf16[192,3352]{1,0:T(8,128)(2,1)}, bf16[384,768]{1,0:T(8,128)(2,1)})) %all-reduce.12.cloned.1.call-update) | async-done | bytes 1877008 | tf_op jit(solution)/shard_map/psum | solution.py:731
  466.1 0.0 copy-start.2
  466.1 3.1 convert_element_type.27
  469.1 0.0 copy-start.1
  469.1 0.0 copy-done.2
  469.1 1.1 convert_element_type.28
  470.2 0.7 copy-done.1
  471.0 0.0 copy-start
  471.0 1.1 copy.28
  472.1 1.3 copy-done
  473.4 1.7 copy.29
  (7 shorter events, 0.0 us)
Async XLA Ops:
  8.0 214.5 %reduce-scatter.5.cloned.1.call-start = ((), (), s32[]{:S(2)}) async-start(), calls=%async_computation.4 | async-start | bytes 2949120 | tf_op jit(solution)/shard_map/reduce_scatter | solution.py:732
  173.3 146.0 %reduce-scatter.3.cloned.1.call-start = ((), (), s32[]{:S(2)}) async-start(), calls=%async_computation.3 | async-start | bytes 6635520 | tf_op jit(solution)/shard_map/reduce_scatter | solution.py:731
  174.0 227.4 %all-reduce.10.cloned.1.call-start = ((), (), s32[]{:S(2)}) async-start(), calls=%async_computation.2 | async-start | bytes 229376 | tf_op jit(solution)/shard_map/psum | solution.py:733
  174.6 291.5 %all-reduce.12.cloned.1.call-start = ((), (), s32[]{:S(2)}) async-start(), calls=%async_computation.5 | async-start | bytes 3833856 | tf_op jit(solution)/shard_map/psum | solution.py:731
  466.1 3.1 copy-start.2
  469.1 1.8 copy-start.1
  471.0 2.5 copy-start
Sparse Core Ops, SparseCore 0:
  173.4 49.0 reduce-scatter.4
  224.8 94.4 reduce-scatter.2
Sparse Core Ops, SparseCore 1:
  180.1 221.3 all-reduce.9
  404.7 61.3 all-reduce.11

commit v2 on v1

--- a/solution.py
+++ b/solution.py
@@ -179,6 +179,200 @@
             self.copy(4, d).wait_recv()
             for kind in range(5):
                 self.copy(kind, d).wait_send()
+
+
+def meet(at, shards, sem):
+    for who in ("one", "two", "mate"):
+        pl.semaphore_signal(sem, inc=1, device_id=(at[who], at["shard"]), device_id_type=MESH)
+    for d in range(1, shards):
+        pl.semaphore_signal(sem, inc=1, device_id=(at["rep"], (at["shard"] + d) % shards), device_id_type=MESH)
+
+
+def met(shards, sem):
+    pl.semaphore_wait(sem, 2 + shards)
+
+
+class Reduce:
+    def __init__(self, at, grad, rows, half, slots, out, column, sems, part, local):
+        self.at, self.grad, self.rows, self.half, self.slots = at, grad, rows, half, slots
+        self.out, self.column = out, column
+        self.tall, self.own_rows = rows // 16, rows // 4
+        self.send, self.recv = (lambda i: sems[0].at[part, i]), (lambda i: sems[1].at[part, i])
+        self.local = local
+        self.keep = pl.ds(pl.multiple_of(at["core"] * half, 128), half)
+        self.give = pl.ds(pl.multiple_of((1 - at["core"]) * half, 128), half)
+
+    def slot(self, level, start, count):
+        ref, row, column = self.slots[level]
+        return ref.at[pl.ds(row + start, count), pl.ds(column, self.half)]
+
+    def at_block(self, shard, a, b):
+        return pl.multiple_of(shard * self.own_rows + (2 * b + a) * self.tall, 16)
+
+    def block(self, shard, a, b):
+        return self.grad.at[pl.ds(self.at_block(shard, a, b), self.tall), self.keep]
+
+    def to(self, src, dst, index, who):
+        rep, shard = who
+        return remote(src, dst, self.send(index), self.recv(index), rep, shard)
+
+    def partner(self, name):
+        return self.at[name], self.at["shard"]
+
+    def add(self, start, level, place_in_slot):
+        rows = pl.ds(start, self.tall)
+        got = self.slot(level, place_in_slot, self.tall)[...]
+        self.grad[rows, self.keep] = (self.grad[rows, self.keep].astype(f32) + got.astype(f32)).astype(bf16)
+
+    def halves(self):
+        whole = self.slot(0, 0, self.rows)
+        return self.to(self.grad.at[:, self.give], whole, 0, self.partner("mate"))
+
+    def begin(self):
+        self.halves().start()
+
+    def first(self):
+        at = self.at
+        self.halves().wait_recv()
+
+        @pl.loop(0, 16)
+        def _(i):
+            start = pl.multiple_of(i * self.tall, 16)
+            self.add(start, 0, start)
+
+        for shard in range(4):
+            for b in range(2):
+                self.to(
+                    self.block(shard, 1 - at["a"], b),
+                    self.slot(1, (2 * shard + b) * self.tall, self.tall),
+                    1,
+                    self.partner("one"),
+                ).start()
+
+    def all_of(self, level, index, name):
+        whole = self.slot(level, 0, self.rows >> level)
+        return self.to(whole, whole, index, self.partner(name))
+
+    def second(self):
+        at = self.at
+        self.all_of(1, 1, "one").wait_recv()
+        for shard in range(4):
+            for b in range(2):
+                self.add(self.at_block(shard, at["a"], b), 1, (2 * shard + b) * self.tall)
+        for shard in range(4):
+            self.to(
+                self.block(shard, at["a"], 1 - at["b"]),
+                self.slot(2, shard * self.tall, self.tall),
+                2,
+                self.partner("two"),
+            ).start()
+
+    def across(self, d):
+        at = self.at
+        shard = (at["shard"] + d) % 4
+        return self.to(
+            self.block(shard, at["a"], at["b"]), self.slot(3, (d - 1) * self.tall, self.tall), 2 + d, (at["rep"], shard)
+        )
+
+    def third(self):
+        at = self.at
+        self.all_of(2, 2, "two").wait_recv()
+        for shard in range(4):
+            self.add(self.at_block(shard, at["a"], at["b"]), 2, shard * self.tall)
+        for d in range(1, 4):
+            self.across(d).start()
+
+    def landed(self, a, b):
+        rows = pl.ds(pl.multiple_of((2 * b + a) * self.tall, 16), self.tall)
+        return self.out.at[rows, pl.ds(pl.multiple_of(self.column + self.at["core"] * self.half, 128), self.half)]
+
+    def spread(self, index):
+        at = self.at
+        own = self.block(at["shard"], at["a"], at["b"])
+        return self.to(own, self.landed(at["a"], at["b"]), index, self.partner("one" if index == 6 else "two"))
+
+    def home(self):
+        at = self.at
+        own = self.block(at["shard"], at["a"], at["b"])
+        return pltpu.make_async_copy(own, self.landed(at["a"], at["b"]), self.local)
+
+    def fourth(self):
+        at = self.at
+        for d in range(1, 4):
+            self.across(d).wait_recv()
+        rows = pl.ds(self.at_block(at["shard"], at["a"], at["b"]), self.tall)
+        total = self.grad[rows, self.keep].astype(f32)
+        for d in range(1, 4):
+            total = total + self.slot(3, (d - 1) * self.tall, self.tall)[...].astype(f32)
+        self.grad[rows, self.keep] = total.astype(bf16)
+        self.spread(7).start()
+        self.spread(6).start()
+        self.home().start()
+
+    def relay(self):
+        at = self.at
+        far = self.landed(at["a"], 1 - at["b"])
+        return self.to(far, far, 8, self.partner("one"))
+
+    def fifth(self):
+        self.spread(7).wait_recv()
+        self.relay().start()
+
+    def strip(self):
+        columns = pl.ds(pl.multiple_of(self.column + self.at["core"] * self.half, 128), self.half)
+        return self.to(self.out.at[:, columns], self.out.at[:, columns], 9, self.partner("mate"))
+
+    def sixth(self):
+        self.home().wait()
+        self.spread(6).wait_recv()
+        self.relay().wait_recv()
+        self.strip().start()
+
+    def seventh(self):
+        self.strip().wait_recv()
+        self.halves().wait_send()
+        self.all_of(1, 1, "one").wait_send()
+        self.all_of(2, 2, "two").wait_send()
+        for d in range(1, 4):
+            self.across(d).wait_send()
+        self.spread(6).wait_send()
+        self.spread(7).wait_send()
+        self.relay().wait_send()
+        self.strip().wait_send()
+
+
+class Total:
+    def __init__(self, at, mine, slots, sems):
+        self.at, self.mine, self.slots, self.sems = at, mine, slots, sems
+
+    def copy(self, index):
+        at = self.at
+        if index < 3:
+            who = at[("mate", "one", "two")[index]], at["shard"]
+        else:
+            who = at["rep"], (at["shard"] + index - 2) % 4
+        return remote(self.mine.at[min(index, 3)], self.slot(index), self.sems[0].at[index], self.sems[1].at[index], *who)
+
+    def slot(self, index):
+        return self.slots.at[index // 3, pl.ds(8 + (index % 3) * 112, 112), :]
+
+    def begin(self):
+        self.copy(0).start()
+
+    def step(self, index):
+        self.copy(index).wait_recv()
+        self.mine[index + 1] = self.mine[index] + self.slot(index)[...]
+        for following in (index + 1,) if index < 2 else (3, 4, 5):
+            self.copy(following).start()
+
+    def finish(self, out):
+        total = self.mine[3]
+        for index in (3, 4, 5):
+            self.copy(index).wait_recv()
+            total = total + self.slot(index)[...]
+        for index in range(6):
+            self.copy(index).wait_send()
+        out[...] = total
 
 
 def spread_lanes(block, width, offset):
@@ -393,7 +587,7 @@
         low_dstate = s["state"][:, cols].astype(bf16)
         s["lowd"][:, cols] = low_dstate
         part = nn(bv, low_dstate) * shrink_e
-        s["part"][:, cols] = part
+        s["part"][:CHUNK, cols] = part
         keep_e = nn(keep_p, s["one64"][:, cols])[0:1, :]
         kept = s["state"][:, cols] * keep_e
         s["tail"][:, cols] = partial_sum(s["xbc"][rows, cols].astype(f32) * part) + partial_sum(
@@ -415,13 +609,13 @@
             e = jnp.exp(jnp.minimum(d, bound))
             weights.append((gram * e).astype(bf16))
             dgram = dgram + dweights[:, half * 128 : (half + 1) * 128] * e
-        dx = nn(jnp.concatenate(weights, axis=1), stack) + s["part"][:, cols]
-        s["part"][:, cols] = xv.astype(f32) * dx
+        dx = nn(jnp.concatenate(weights, axis=1), stack) + s["part"][:CHUNK, cols]
+        s["part"][:CHUNK, cols] = xv.astype(f32) * dx
         dx = dx + sm[7:8, cols] * dy.astype(f32)
         pre = s["pre"][rows, cols].astype(f32)
         sg = sigmoid(pre)
         s["pre"][rows, cols] = (dx * (sg * (1.0 + pre * (1.0 - sg)))).astype(bf16)
-    high, low = two_parts(s["part"][...])
+    high, low = two_parts(s["part"][:CHUNK, :])
     colsum = nn(high, s["sum64"][...]) + nn(low, s["sum64"][...])
     high, low = two_parts(s["tail"][...])
     dlast = jnp.sum(nn(high, s["sum64"][...]) + nn(low, s["sum64"][...]), axis=0, keepdims=True)
@@ -505,7 +699,11 @@
     dys=((CHUNK, INNER), bf16),
     xw=((CHUNK, INNER), bf16),
     lowd=((CHUNK, INNER), bf16),
-    part=((CHUNK, INNER), f32),
+    dwz=((MODEL, INNER), bf16),
+    dwu=((MODEL, 2048), bf16),
+    dwo=((INNER, MODEL), bf16),
+    zr=((1488, MODEL), bf16),
+    mine=((4, 112, 256), f32),
     up=((2, 8 + LEN, 256), f32),
     state=((STATE, INNER), f32),
     states=((SEQ * LEN // CHUNK, STATE, INNER), bf16),
@@ -570,6 +768,7 @@
         part.share()
     for part in (gate_part, out_part):
         part.finish()
+    return at
 
 
 def copy_weights(seg_ref, win_all, wout_all, sm_all, hd, s, sems):
@@ -585,29 +784,69 @@
     s["sm"][7:8, :] = hd[2:3, :]
 
 
+def transposed(src, dst):
+    for i in range(TOKENS // 128):
+        for j in range(MODEL // 128):
+            dst[j * 128 : (j + 1) * 128, i * 128 : (i + 1) * 128] = src[
+                i * 128 : (i + 1) * 128, j * 128 : (j + 1) * 128
+            ].T
+
+
+def out_weight_gradient(cot_ref, s):
+    for j in range(QUADS):
+        cols = slice(j * 256, (j + 1) * 256)
+        s["dwo"][cols, :] = tn(s["gated"][:, cols], cot_ref[...]).astype(bf16)
+
+
+def in_weight_gradient(ref, column, tile):
+    def fill(turned):
+        for i in range(3):
+            rows = slice(i * 256, (i + 1) * 256)
+            ref[rows, column : column + tile.shape[1]] = nn(turned[rows, :TOKENS], tile[...]).astype(bf16)
+
+    return fill
+
+
+def token_gradient(i, win, gtok_ref, s):
+    rows = pl.ds(pl.multiple_of(i * 256, 256), 256)
+    for j in range(3):
+        cols = slice(j * 256, (j + 1) * 256)
+        gtok_ref[rows, cols] = (
+            nt(s["dz"][rows, :], win[cols, :INNER])
+            + nt(s["u"][rows, :], win[cols, INNER:DT])
+            + nt(s["ddt"][rows, :], win[cols, DT : DT + 128])
+        )
+
+
+def pack_small(mine, s):
+    for j in range(CONV_CH // 256):
+        sums = [jnp.sum(s["acc"][k, :, j * 256 : (j + 1) * 256], axis=0, keepdims=True) for k in range(10)]
+        mine[0, j * 16 : (j + 1) * 16, :] = jnp.concatenate(sums + [jnp.zeros((6, 256), f32)], axis=0)
+
+
 def layer_kernel(
-    direct,
-    shards,
-    x_ref,
-    cot_ref,
-    seg_ref,
-    win_own,
-    wout_own,
-    sm_own,
-    hd,
-    mixed_ref,
-    gtok_ref,
-    dwin_ref,
-    dwout_ref,
-    gsm_ref,
-    *refs,
+    direct, shards, x_ref, cot_ref, seg_ref, win_own, wout_own, sm_own, hd, mixed_ref, gtok_ref, gin_ref, gout_ref, gsm_ref, *refs
 ):
     s = dict(zip(SCRATCH, refs))
     s["mixed_sem"], *sems = refs[len(SCRATCH) :]
     s["y"] = gtok_ref
+    s["part"] = s["z"]
     win, wout, sm = s["win"], s["wout"], s["sm"]
     if direct:
-        gather_weights(shards, seg_ref, win_own, wout_own, sm_own, hd, s, *sems)
+        *sems, sends, recvs, locals_, total_send, total_recv, forward_done, scan_done = sems
+        at = gather_weights(shards, seg_ref, win_own, wout_own, sm_own, hd, s, *sems)
+        pair = (sends, recvs)
+        zr, xbc, dy = s["zr"], s["xbc"], s["dy"]
+        gate_sum = Reduce(
+            at, s["dwz"], MODEL, INNER // 2, [(zr, 0, 0), (zr, 768, 0), (zr, 1152, 0), (zr, 1344, 0)], gin_ref, 0, pair, 0, locals_.at[0]
+        )
+        out_sum = Reduce(
+            at, s["dwo"], INNER, MODEL // 2, [(wout, 0, 0), (wout, 0, 384), (wout, 768, 384), (wout, 1152, 384)], gout_ref, 0, pair, 1, locals_.at[1]
+        )
+        conv_sum = Reduce(
+            at, s["dwu"], MODEL, 1024, [(xbc, 0, 0), (dy, 0, 0), (dy, 384, 0), (dy, 576, 0)], gin_ref, INNER, pair, 2, locals_.at[2]
+        )
+        small_sum = Total(at, s["mine"], s["up"], (total_send, total_recv))
     else:
         copy_weights(seg_ref, win_own, wout_own, sm_own, hd, s, *sems)
     chunks = LEN // CHUNK
@@ -625,51 +864,94 @@
         def _(i):
             gate(q, i, x_ref, cot_ref, win, wout, sm, mixed_ref, s)
 
+    if direct:
+        meet(at, shards, forward_done)
+    out_weight_gradient(cot_ref, s)
+    if direct:
+        met(shards, forward_done)
+        out_sum.begin()
+    turned = s["gated"]
+    transposed(s["nrm"], turned)
     for j in range(QUADS):
-        cols = slice(j * 256, (j + 1) * 256)
-        dwout_ref[cols, :] = tn(s["gated"][:, cols], cot_ref[...]).astype(bf16)
+        in_weight_gradient(s["dwz"], j * 256, s["dz"].at[:, j * 256 : (j + 1) * 256])(turned)
+    if direct:
+        gate_sum.begin()
+
+    @pl.loop(0, SEQ * chunks)
+    def _(n):
+        @pl.when(n % chunks == 0)
+        def _():
+            s["state"][...] = jnp.zeros((STATE, INNER), f32)
+
+        scan_backward(n // chunks, chunks - 1 - n % chunks, seg_ref, sm, hd, s)
+        if direct:
+            stages = ((0, "first"), (2, "second"), (4, "third"), (6, "fourth"), (7, "fifth"))
+            for index, name in stages:
+
+                @pl.when(n == index)
+                def _():
+                    getattr(out_sum, name)()
+                    getattr(gate_sum, name)()
+
+    if direct:
+        meet(at, shards, scan_done)
+        out_sum.sixth()
+        gate_sum.sixth()
 
     @pl.loop(0, SEQ)
     def _(q):
-        s["state"][...] = jnp.zeros((STATE, INNER), f32)
-
-        @pl.loop(0, chunks)
-        def _(c):
-            scan_backward(q, chunks - 1 - c, seg_ref, sm, hd, s)
-
         conv_backward(q, sm, s)
 
-    turned = s["gated"]
-    for i in range(TOKENS // 128):
-        for j in range(MODEL // 128):
-            turned[j * 128 : (j + 1) * 128, i * 128 : (i + 1) * 128] = s["nrm"][
-                i * 128 : (i + 1) * 128, j * 128 : (j + 1) * 128
-            ].T
-    for j in range(13):
-        cols = slice(j * 256, (j + 1) * 256)
-        of = s["dz"][:, cols] if j < QUADS else s["u"][:, j * 256 - INNER : (j + 1) * 256 - INNER]
-        for i in range(3):
-            rows = slice(i * 256, (i + 1) * 256)
-            dwin_ref[rows, cols] = nn(turned[rows, :TOKENS], of).astype(bf16)
-    dwin_ref[:, 3328:] = nn(turned[:MODEL, :TOKENS], s["ddt"][...]).astype(bf16)[:, :HEADS]
-
-    @pl.loop(0, TOKENS // 256)
-    def _(i):
-        rows = pl.ds(pl.multiple_of(i * 256, 256), 256)
-        for j in range(3):
-            cols = slice(j * 256, (j + 1) * 256)
-            gtok_ref[rows, cols] = (
-                nt(s["dz"][rows, :], win[cols, :INNER])
-                + nt(s["u"][rows, :], win[cols, INNER : INNER + CONV_CH])
-                + nt(s["ddt"][rows, :], win[cols, DT : DT + 128])
-            )
+    for j in range(CONV_CH // 256):
+        in_weight_gradient(s["dwu"], j * 256, s["u"].at[:, j * 256 : (j + 1) * 256])(turned)
+    in_weight_gradient(s["dwu"], CONV_CH, s["ddt"])(turned)
+    s["dwu"][:, CONV_CH + 128 :] = jnp.zeros((MODEL, 128), bf16)
+    if direct:
+        met(shards, scan_done)
+        conv_sum.begin()
+        token_gradient(0, win, gtok_ref, s)
+        conv_sum.first()
+
+        @pl.loop(1, TOKENS // 256)
+        def _(i):
+            token_gradient(i, win, gtok_ref, s)
+
+        conv_sum.second()
+    else:
+
+        @pl.loop(0, TOKENS // 256)
+        def _(i):
+            token_gradient(i, win, gtok_ref, s)
 
     @pl.loop(0, TOKENS // 128)
     def _(i):
         input_gradient(i, x_ref, cot_ref, sm, gtok_ref, s)
 
-    for k in range(10):
-        gsm_ref[k : k + 1, :] = jnp.sum(s["acc"][k], axis=0, keepdims=True)
+    pack_small(s["mine"], s)
+    if direct:
+        small_sum.begin()
+        conv_sum.third()
+        small_sum.step(0)
+        out_sum.seventh()
+        gate_sum.seventh()
+        small_sum.step(1)
+        conv_sum.fourth()
+        small_sum.step(2)
+        conv_sum.fifth()
+        conv_sum.sixth()
+        small_sum.finish(gsm_ref)
+        conv_sum.seventh()
+    else:
+        gsm_ref[...] = s["mine"][0]
+        copies = [
+            pltpu.make_async_copy(s["dwz"], gin_ref.at[:, :INNER], sems[0].at[0]),
+            pltpu.make_async_copy(s["dwu"], gin_ref.at[:, INNER:], sems[0].at[1]),
+            pltpu.make_async_copy(s["dwo"], gout_ref, sems[0].at[2]),
+        ]
+        for copy in copies:
+            copy.start()
+        for copy in copies:
+            copy.wait()
 
 
 def reaches(mesh):
@@ -683,6 +965,8 @@
     dma = pltpu.SemaphoreType.DMA
     if direct:
         sems = [dma((3, 5, shards)), dma((3, 5, shards)), dma((shards,)), dma((shards,))]
+        sems += [dma((3, 10)), dma((3, 10)), dma((3,)), dma((6,)), dma((6,))]
+        sems += [pltpu.SemaphoreType.REGULAR] * 2
         options = dict(collective_id=0, has_side_effects=True)
         weights = vmem
     else:
@@ -692,12 +976,12 @@
         out_shape=(
             jax.ShapeDtypeStruct((TOKENS, MODEL), bf16),
             jax.ShapeDtypeStruct((TOKENS, MODEL), f32),
-            jax.ShapeDtypeStruct((MODEL, PROJ), bf16),
-            jax.ShapeDtypeStruct((INNER, MODEL), bf16),
-            jax.ShapeDtypeStruct((10, CONV_CH), f32),
+            jax.ShapeDtypeStruct((MODEL // shards if direct else MODEL, PADDED), bf16),
+            jax.ShapeDtypeStruct((INNER // shards if direct else INNER, MODEL), bf16),
+            jax.ShapeDtypeStruct((112, 256), f32),
         ),
         in_specs=[vmem] * 3 + [weights] * 3 + [vmem],
-        out_specs=[hbm] + [vmem] * 4,
+        out_specs=[hbm, vmem, hbm, hbm, vmem],
         scratch_shapes=[pltpu.VMEM(shape, kind) for shape, kind in SCRATCH.values()] + [dma] + sems,
         compiler_params=pltpu.CompilerParams(vmem_limit_bytes=67043328, **options),
         name="layer",
@@ -724,13 +1008,15 @@
         [rows_to_lanes(v, CONV_CH) for v in (dt_bias, a_log, jnp.repeat(d_skip, HEADDIM))] + [jnp.zeros((5, CONV_CH), f32)],
         axis=0,
     )
-    mixed, gtok, dwin, dwout, gsm = layer(
+    mixed, gtok, gin, gout, gsm = layer(
         mesh,
         tokens.reshape(TOKENS, MODEL), cotangent.reshape(TOKENS, MODEL), segment_ids, win, wout, sm, hd
     )
-    dwin = lax.psum(lax.psum_scatter(dwin, "shard", scatter_dimension=0, tiled=True), "rep")
-    dwout = lax.psum(lax.psum_scatter(dwout, "shard", scatter_dimension=0, tiled=True), "rep")
-    gsm = lax.psum(gsm, ("rep", "shard"))
+    if not reaches(mesh):
+        gin = lax.psum(lax.psum_scatter(gin, "shard", scatter_dimension=0, tiled=True), "rep")
+        gout = lax.psum(lax.psum_scatter(gout, "shard", scatter_dimension=0, tiled=True), "rep")
+        gsm = lax.psum(gsm, ("rep", "shard"))
+    gsm = gsm.reshape(CONV_CH // 256, 16, 256).transpose(1, 0, 2).reshape(16, CONV_CH)
     me = lax.axis_index("shard")
 
     def owned(v, like):
@@ -740,14 +1026,14 @@
         mixed.reshape(SEQ, LEN, MODEL),
         gtok.reshape(SEQ, LEN, MODEL),
         owned(gsm[6, :MODEL], norm_gain),
-        dwin.astype(f32),
+        gin[:, :PROJ].astype(f32),
         owned(gsm[:CONV].T, conv_weight),
         owned(gsm[4], conv_bias),
         gsm[8, :HEADS],
         gsm[9, :HEADS],
         gsm[7, :INNER].reshape(HEADS, HEADDIM).sum(axis=1),
         owned(gsm[5, :INNER], gate_gain),
-        dwout.astype(f32),
+        gout.astype(f32),
     )
 
 

time: 483 us -> 237 us (0.49)
  waiting for transfers between devices: 285 us -> 0 us
  Pallas kernels: 159 us -> 215 us
  between operations: 15.5 us -> 0.7 us
    reduce_scatter x2 -> x0, waiting for transfers between devices: 145 us -> none  [the longest x1 96.8 us: on_device(): lax.psum_scatter(dwin, 'shard', scatter_dimension=0, tiled=True)]
    psum x2 -> x0, waiting for transfers between devices: 139 us -> none  [the longest x1 82.1 us: on_device(): gsm = lax.psum(gsm, ('rep', 'shard'))]
    pallas_call x1, Pallas kernels: 159 us -> 215 us  [layer(): pl.pallas_call(partial(layer_kernel, direct, shards), out_shape=(jax.Shap...]
  transfers between devices with their start and end apart: 4 -> 0, of which waited for: 4 -> 0; matrix products, arithmetic and copies ran while one was open for 2% -> 0% of each run, Pallas kernels for 0% -> 0%
where the time goes in v2:
time: 237 us; the launch traced here: 236 us
  Pallas kernels  215 us (91%)
  local copies, waits for them, and re-layouts  14.9 us (6%)
  other arithmetic  6.09 us (3%)
    pallas_call x1, Pallas kernels, layer(): pl.pallas_call(partial(layer_kernel, direct, shards), out_shape=(jax.Shap...  215 us
    unnamed x11, local copies, waits for them, and re-layouts  5.79 us

profile of v2, /device:TPU:0, one launch (start us, length us, event | category | flops | bytes accessed | tf_op | source)
XLA Modules:
  0.0 236.4 jit_solution(626840551959315721)
XLA Ops:
  0.6 0.7 broadcast_in_dim.33
  1.4 0.1 reshape.50
  1.5 0.7 pad.32
  2.1 0.7 pad.33
  2.8 0.1 pad.38.clone
  2.9 0.7 maximum_maximum_fusion.hd
  3.6 0.7 pad.28
  4.3 0.7 pad.29
  4.9 0.7 broadcast_in_dim.28
  5.6 0.7 concatenate.7
  6.3 0.6 pad_convert_fusion.sm_own
  6.9 214.7 %layer.1 = (bf16[1024,768]{1,0:T(8,128)(2,1)}, f32[1024,768]{1,0:T(8,128)}, bf16[192,3584]{1,0:T(8,128)(2,1)}, bf16[384,768]{1,0:T(8,128)(2,1)}, f32[112,256]{1,0:T(8,128)}) custom-call(bf16[1024,768]{1,0:T(8,128)(2,1)} %bitcast.25, bf16[1024,768]{1,0:T(8,128)(2,1)} %bitcast.26, s32[2,512]{1,0:T(2,128)} %seg_ref.1, bf16[192,3352]{1,0:T(8,128)(2,1)} %win_own.1, ...), custom_call_target="tpu_custom_call" | custom-call | tf_op jit(solution)/shard_map/layer/pallas_call | solution.py:974
  221.7 0.9 copy.26
  222.6 0.6 dynamic-slice_reduce_fusion
  223.2 1.0 copy.30
  224.2 0.7 dynamic-slice_bitcast_fusion
  224.9 0.7 dynamic_slice.19
  225.6 0.6 constant_dynamic-slice_fusion
  226.2 0.1 reshape_squeeze.3
  226.3 0.6 reduce_sum.9
  226.9 0.5 slice_bitcast_fusion.1
  227.4 0.0 copy-start.2
  227.4 3.1 %slice_convert_fusion = f32[192,3352]{1,0:T(8,128)} fusion(bf16[192,3584]{1,0:T(8,128)(2,1)} %get-tuple-element.19), kind=kLoop, calls=%fused_computation | loop fusion | flops 643584 | bytes 3861504 | tf_op jit(solution)/shard_map/convert_element_type | solution.py:1029
  230.5 0.0 copy-start.1
  230.5 0.0 copy-done.2
  230.5 1.1 convert_element_type.28
  231.6 0.7 copy-done.1
  232.3 0.0 copy-start
  232.3 1.1 copy.33
  233.5 1.3 copy-done
  234.8 1.7 copy.34
  (13 shorter events, 0.1 us)
Async XLA Ops:
  227.4 3.1 %copy-start.2 = (bf16[384,768]{1,0:T(8,128)(2,1)S(1)}, bf16[384,768]{1,0:T(8,128)(2,1)}, u32[]{:S(2)}) copy-start(bf16[384,768]{1,0:T(8,128)(2,1)} %get-tuple-element.20) | copy-start | bytes 1769476
  230.5 1.8 copy-start.1
  232.3 2.5 %copy-start = (f32[1024,768]{1,0:T(8,128)S(1)}, f32[1024,768]{1,0:T(8,128)}, u32[]{:S(2)}) copy-start(f32[1024,768]{1,0:T(8,128)} %get-tuple-element.17) | copy-start | bytes 9437188

commit v3 on v2

--- a/solution.py
+++ b/solution.py
@@ -78,10 +78,8 @@
     return high, (a - high.astype(f32)).astype(bf16)
 
 
-def y_at(row, count, cols):
-    right = cols.start >= MODEL
-    base, shift = (LEN, MODEL) if right else (0, 0)
-    return pl.ds(pl.multiple_of(base + row, 8), count), slice(cols.start - shift, cols.stop - shift)
+def scanned(s, rows, cols):
+    return s["dy"][rows, cols].astype(f32) + s["dz"][rows, cols].astype(f32)
 
 
 def place():
@@ -97,6 +95,7 @@
         a=a,
         b=b,
         one=rep + (1 - 2 * a) * (2 + 2 * core),
+        far=rep + (1 - 2 * a) * (2 + 2 * core) + (1 - 2 * b) * (4 - 2 * core),
         two=rep + (1 - 2 * b) * (4 - 2 * core),
         mate=rep + 1 - 2 * core,
     )
@@ -104,13 +103,13 @@
 
 def greet(at, shards):
     barrier = pltpu.get_barrier_semaphore()
-    for who in ("one", "two", "mate"):
+    for who in ("one", "two", "far", "mate"):
         pl.semaphore_signal(barrier, inc=1, device_id=(at[who], at["shard"]), device_id_type=MESH)
     for d in range(1, shards):
         pl.semaphore_signal(
             barrier, inc=1, device_id=(at["rep"], (at["shard"] + d) % shards), device_id_type=MESH
         )
-    pl.semaphore_wait(barrier, 2 + shards)
+    pl.semaphore_wait(barrier, 3 + shards)
 
 
 def remote(src, dst, send, recv, rep, shard):
@@ -182,14 +181,14 @@
 
 
 def meet(at, shards, sem):
-    for who in ("one", "two", "mate"):
+    for who in ("one", "two", "far", "mate"):
         pl.semaphore_signal(sem, inc=1, device_id=(at[who], at["shard"]), device_id_type=MESH)
     for d in range(1, shards):
         pl.semaphore_signal(sem, inc=1, device_id=(at["rep"], (at["shard"] + d) % shards), device_id_type=MESH)
 
 
 def met(shards, sem):
-    pl.semaphore_wait(sem, 2 + shards)
+    pl.semaphore_wait(sem, 3 + shards)
 
 
 class Reduce:
@@ -289,7 +288,7 @@
     def spread(self, index):
         at = self.at
         own = self.block(at["shard"], at["a"], at["b"])
-        return self.to(own, self.landed(at["a"], at["b"]), index, self.partner("one" if index == 6 else "two"))
+        return self.to(own, self.landed(at["a"], at["b"]), index, self.partner(("one", "two", "far")[index - 6]))
 
     def home(self):
         at = self.at
@@ -305,18 +304,9 @@
         for d in range(1, 4):
             total = total + self.slot(3, (d - 1) * self.tall, self.tall)[...].astype(f32)
         self.grad[rows, self.keep] = total.astype(bf16)
-        self.spread(7).start()
-        self.spread(6).start()
+        for index in (8, 7, 6):
+            self.spread(index).start()
         self.home().start()
-
-    def relay(self):
-        at = self.at
-        far = self.landed(at["a"], 1 - at["b"])
-        return self.to(far, far, 8, self.partner("one"))
-
-    def fifth(self):
-        self.spread(7).wait_recv()
-        self.relay().start()
 
     def strip(self):
         columns = pl.ds(pl.multiple_of(self.column + self.at["core"] * self.half, 128), self.half)
@@ -324,8 +314,8 @@
 
     def sixth(self):
         self.home().wait()
-        self.spread(6).wait_recv()
-        self.relay().wait_recv()
+        for index in (6, 7, 8):
+            self.spread(index).wait_recv()
         self.strip().start()
 
     def seventh(self):
@@ -335,15 +325,24 @@
         self.all_of(2, 2, "two").wait_send()
         for d in range(1, 4):
             self.across(d).wait_send()
-        self.spread(6).wait_send()
-        self.spread(7).wait_send()
-        self.relay().wait_send()
+        for index in (6, 7, 8):
+            self.spread(index).wait_send()
         self.strip().wait_send()
 
 
+def unpack_small(total, gain, out):
+    for j in range(CONV_CH // 256):
+        out[0:8, j * 256 : (j + 1) * 256] = total[j * 8 : (j + 1) * 8, :]
+    for j in range(MODEL // 128):
+        out[6:7, j * 128 : (j + 1) * 128] = gain[j : j + 1, :]
+    for k in range(3):
+        out[7 + k : 8 + k, 0:128] = total[8 * (k // 2) + 6 : 8 * (k // 2) + 7, (k % 2) * 128 : (k % 2 + 1) * 128]
+
+
 class Total:
-    def __init__(self, at, mine, slots, sems):
-        self.at, self.mine, self.slots, self.sems = at, mine, slots, sems
+    def __init__(self, at, mine, slot, sems, part):
+        self.at, self.mine, self.slot = at, mine, slot
+        self.send, self.recv = (lambda i: sems[0].at[part, i]), (lambda i: sems[1].at[part, i])
 
     def copy(self, index):
         at = self.at
@@ -351,10 +350,7 @@
             who = at[("mate", "one", "two")[index]], at["shard"]
         else:
             who = at["rep"], (at["shard"] + index - 2) % 4
-        return remote(self.mine.at[min(index, 3)], self.slot(index), self.sems[0].at[index], self.sems[1].at[index], *who)
-
-    def slot(self, index):
-        return self.slots.at[index // 3, pl.ds(8 + (index % 3) * 112, 112), :]
+        return remote(self.mine.at[min(index, 3)], self.slot(index), self.send(index), self.recv(index), *who)
 
     def begin(self):
         self.copy(0).start()
@@ -365,14 +361,14 @@
         for following in (index + 1,) if index < 2 else (3, 4, 5):
             self.copy(following).start()
 
-    def finish(self, out):
+    def finish(self):
         total = self.mine[3]
         for index in (3, 4, 5):
             self.copy(index).wait_recv()
             total = total + self.slot(index)[...]
         for index in range(6):
             self.copy(index).wait_send()
-        out[...] = total
+        return total
 
 
 def spread_lanes(block, width, offset):
@@ -407,19 +403,23 @@
             s["segc"][q, 8 + i * 128 : 8 + (i + 1) * 128, :] = jnp.broadcast_to(seg, (128, 128)).T
 
 
-def project(q, x_ref, seg_ref, win, sm, hd, s):
-    row0 = pl.multiple_of(q * LEN, LEN)
-    for i in range(LEN // 128):
-        rows = pl.ds(row0 + i * 128, 128)
+def norm_input(q, x_ref, sm, s):
+    @pl.loop(0, LEN // 64)
+    def _(i):
+        rows = pl.ds(pl.multiple_of(q * LEN + i * 64, 64), 64)
         x = x_ref[rows, :].astype(f32)
         r = lax.rsqrt(jnp.mean(x * x, axis=1, keepdims=True) + EPS)
         s["nrm"][rows, :] = (x * r * sm[6:7, :MODEL]).astype(bf16)
+
+
+def project(q, win, sm, hd, s):
+    row0 = pl.multiple_of(q * LEN, LEN)
     seg = s["segc"][q, 8 : 8 + LEN, :]
     place = rows_of((LEN, 128))
     for o in range(1, CONV):
         s["back"][o - 1] = ((seg == pltpu.roll(seg, o, 0)) & (place >= o)).astype(f32)
     rows = pl.ds(row0, LEN)
-    raw = nn(s["nrm"][rows, :], win[:, DT : DT + 128]) + hd[0:1, :128]
+    raw = nn(s["nrm"][rows, :], win[:, DT : DT + 128]) + hd[0:1, :]
     s["dtx"][rows, :] = raw
     for j in range(CONV_CH // 256):
         slot = j % 2
@@ -445,7 +445,7 @@
     rows = pl.ds(row0, CHUNK)
     raw = s["dtx"][rows, :]
     dt = jnp.maximum(raw, 0.0) + jnp.log1p(jnp.exp(-jnp.abs(raw)))
-    rate = -jnp.exp(hd[1:2, :128]) * dt
+    rate = -jnp.exp(hd[1:2, :]) * dt
     lower = (rows_of((CHUNK, CHUNK)) >= lanes_of((CHUNK, CHUNK))).astype(f32)
     cum = exact(lower, rate)
     source = cum - jnp.log(jnp.maximum(dt, 1e-37))
@@ -501,14 +501,12 @@
             zero = jnp.zeros_like(x2)
             stack = jnp.concatenate([jnp.where(left, x2, zero), jnp.where(left, zero, x2)], axis=0)
             parts.append(nn(jnp.concatenate(weights, axis=1), stack))
-        s["y"][y_at(c * CHUNK, CHUNK, cols)] = (
-            jnp.concatenate(parts, axis=1) + y_state * grow_e
-        )
-
-
-def gate(q, i, x_ref, cot_ref, win, wout, sm, mixed_ref, s):
+        s["dy"][rows, cols], s["dz"][rows, cols] = two_parts(jnp.concatenate(parts, axis=1) + y_state * grow_e)
+
+
+def gate(i, x_ref, cot_ref, win, wout, sm, mixed_ref, s):
     tall, block = 256, 64
-    row0 = q * LEN + i * tall
+    row0 = i * tall
     rows = pl.ds(pl.multiple_of(row0, tall), tall)
     for j in range(QUADS):
         cols = slice(j * 256, (j + 1) * 256)
@@ -518,14 +516,13 @@
     @pl.loop(0, tall // block)
     def _(b):
         own = pl.ds(pl.multiple_of(b * block, block), block)
-        here = i * tall + b * block
         where = pl.ds(pl.multiple_of(row0 + b * block, block), block)
         square = jnp.zeros((block, 128), f32)
         along = jnp.zeros((block, 128), f32)
         for j in range(INNER // 128):
             cols = slice(j * 128, (j + 1) * 128)
             z = s["z"][own, cols]
-            y = s["y"][y_at(here, block, cols)] + sm[7:8, cols] * s["xbc"][where, cols].astype(f32)
+            y = scanned(s, where, cols) + sm[7:8, cols] * s["xbc"][where, cols].astype(f32)
             v = y * (z * sigmoid(z))
             square = square + v * v
             along = along + s["dg"][own, cols] * sm[5:6, cols] * v
@@ -535,7 +532,7 @@
             cols = slice(j * 128, (j + 1) * 128)
             z = s["z"][own, cols]
             dg = s["dg"][own, cols]
-            ys = s["y"][y_at(here, block, cols)]
+            ys = scanned(s, where, cols)
             xv = s["xbc"][where, cols].astype(f32)
             y = ys + sm[7:8, cols] * xv
             sg = sigmoid(z)
@@ -562,7 +559,16 @@
     out.wait()
 
 
-def scan_backward(q, c, seg_ref, sm, hd, s):
+def set_aside(s, at, kind):
+    row, column = (at // 4) * 128, ((at % 4) * 3 + kind) * 128
+    return s["dg"].at[pl.ds(pl.multiple_of(row, 128), 128), pl.ds(pl.multiple_of(column, 128), 128)]
+
+
+def sums_aside(s, at):
+    return s["z"].at[128:256, pl.ds(pl.multiple_of(at * 128, 128), 128)]
+
+
+def scan_backward(q, c, quads, first, seg_ref, sm, hd, s):
     rows, raw, dt, rate, cum, source, segc, segr, grow, shrink, keep = chunk_terms(q, c, seg_ref, hd, s)
     k, t = rows_of((CHUNK, CHUNK)), lanes_of((CHUNK, CHUNK))
     allowed = (segc == segr) & (t >= k)
@@ -577,8 +583,8 @@
     ct = cv.T
     at = q * (LEN // CHUNK) + c
     left = lanes_of((CHUNK, 128)) < HEADDIM
-    dgram = jnp.zeros((CHUNK, CHUNK), f32)
-    for j in range(QUADS):
+    dgram = jnp.zeros((CHUNK, CHUNK), f32) if first else set_aside(s, at, 0)[...]
+    for j in quads:
         cols = slice(j * 256, (j + 1) * 256)
         grow_e = nn(grow_p, s["one64"][:, cols])
         s["dys"][:, cols] = (s["dy"][rows, cols].astype(f32) * grow_e).astype(bf16)
@@ -594,7 +600,7 @@
             kept * s["states"][at, :, cols].astype(f32)
         )
         s["state"][:, cols] = kept + nn(ct, s["dys"][:, cols])
-    for j in range(INNER // 128):
+    for j in range(2 * quads[0], 2 * quads[-1] + 2):
         cols = slice(j * 128, (j + 1) * 128)
         xv = s["xbc"][rows, cols]
         dy = s["dy"][rows, cols]
@@ -615,12 +621,21 @@
         pre = s["pre"][rows, cols].astype(f32)
         sg = sigmoid(pre)
         s["pre"][rows, cols] = (dx * (sg * (1.0 + pre * (1.0 - sg)))).astype(bf16)
-    high, low = two_parts(s["part"][:CHUNK, :])
-    colsum = nn(high, s["sum64"][...]) + nn(low, s["sum64"][...])
-    high, low = two_parts(s["tail"][...])
-    dlast = jnp.sum(nn(high, s["sum64"][...]) + nn(low, s["sum64"][...]), axis=0, keepdims=True)
-    dc = nt(s["dys"][...], s["states"][at])
-    db = nt(s["xw"][...], s["lowd"][...])
+    some = slice(quads[0] * 256, (quads[-1] + 1) * 256)
+    high, low = two_parts(s["part"][:CHUNK, some])
+    colsum = nn(high, s["sum64"][some, :]) + nn(low, s["sum64"][some, :])
+    high, low = two_parts(s["tail"][:, some])
+    dlast = nn(high, s["sum64"][some, :]) + nn(low, s["sum64"][some, :])
+    dc = nt(s["dys"][:, some], s["states"][at, :, some])
+    db = nt(s["xw"][:, some], s["lowd"][:, some])
+    if first:
+        for index, value in enumerate((dgram, db, dc)):
+            set_aside(s, at, index)[...] = value
+        sums_aside(s, at)[...] = colsum
+        s["kept_last"][at] = dlast
+        return
+    db, dc, colsum = db + set_aside(s, at, 1)[...], dc + set_aside(s, at, 2)[...], colsum + sums_aside(s, at)[...]
+    dlast = jnp.sum(dlast + s["kept_last"][at], axis=0, keepdims=True)
     low_dgram = dgram.astype(bf16)
     db = db + nn(low_dgram, cv)
     dc = dc + tn(low_dgram, bv)
@@ -633,21 +648,21 @@
     drate = exact(allowed.astype(f32), dcum) + dlast * (segc == segc[CHUNK - 1 : CHUNK]).astype(f32)
     sg = sigmoid(raw)
     ratio = jnp.where(dt > 1e-30, sg / jnp.maximum(dt, 1e-30), 1.0)
-    draw = colsum * ratio - drate * jnp.exp(hd[1:2, :128]) * sg
+    draw = colsum * ratio - drate * jnp.exp(hd[1:2, :]) * sg
     draw = jnp.where(lanes_of((CHUNK, 128)) < HEADS, draw, 0.0)
     s["ddt"][rows, :] = draw.astype(bf16)
     s["acc"][8, :, 0:128] += partial_sum(draw)
     s["acc"][9, :, 0:128] += partial_sum(drate * rate)
 
 
-def conv_backward(q, sm, s):
+def conv_backward(q, tiles, sm, s):
     row0 = pl.multiple_of(q * LEN, LEN)
     rows = pl.ds(row0, LEN)
     seg = s["segc"][q, 8 : 8 + LEN, :]
     place = rows_of((LEN, 128))
     for o in range(1, CONV):
         s["back"][o - 1] = ((seg == pltpu.roll(seg, LEN - o, 0)) & (place < LEN - o)).astype(f32)
-    for j in range(CONV_CH // 128):
+    for j in tiles:
         cols = slice(j * 128, (j + 1) * 128)
         sums = [jnp.zeros((8, 128), f32)] * 5
         for i in range(LEN // 128):
@@ -668,7 +683,7 @@
 
 
 def input_gradient(i, x_ref, cot_ref, sm, gtok_ref, s):
-    rows = pl.ds(pl.multiple_of(i * 128, 128), 128)
+    rows = pl.ds(pl.multiple_of(i * 64, 64), 64)
     x = x_ref[rows, :].astype(f32)
     dn = gtok_ref[rows, :]
     r = lax.rsqrt(jnp.mean(x * x, axis=1, keepdims=True) + EPS)
@@ -682,7 +697,8 @@
     win=((MODEL, PADDED), bf16),
     wout=((INNER, MODEL), bf16),
     parts=((4, 8, 512), f32),
-    sm=((8, CONV_CH), f32),
+    sm=((16, CONV_CH), f32),
+    hd=((8, 128), f32),
     mixed=((256, MODEL), bf16),
     nrm=((TOKENS, MODEL), bf16),
     u=((TOKENS, CONV_CH), bf16),
@@ -703,12 +719,15 @@
     dwu=((MODEL, 2048), bf16),
     dwo=((INNER, MODEL), bf16),
     zr=((1488, MODEL), bf16),
-    mine=((4, 112, 256), f32),
+    mine=((4, 56, 256), f32),
+    gain=((4, 8, 128), f32),
+    gain_slots=((6, 8, 128), f32),
     up=((2, 8 + LEN, 256), f32),
     state=((STATE, INNER), f32),
     states=((SEQ * LEN // CHUNK, STATE, INNER), bf16),
     rowv=((128, 128), f32),
     tail=((8, INNER), f32),
+    kept_last=((SEQ * LEN // CHUNK, 8, 128), f32),
     segc=((SEQ, 8 + LEN, 128), f32),
     back=((CONV - 1, LEN, 128), f32),
     one128=((128, HEADS * 128), bf16),
@@ -718,15 +737,19 @@
 )
 
 
-def gather_weights(shards, seg_ref, win_own, wout_own, sm_own, hd, s, send_sems, recv_sems, small_send, small_recv):
+def gather_weights(shards, x_ref, seg_ref, win_own, wout_own, sm_own, hd, s, send_sems, recv_sems, small_send, small_recv):
     win, wout, sm = s["win"], s["wout"], s["sm"]
     at = place()
     shard = at["shard"]
     rows = pl.ds(pl.multiple_of(shard * (MODEL // shards), 16), MODEL // shards)
     win[rows, DT:] = jnp.zeros((MODEL // shards, PADDED - DT), bf16)
     win[rows, :PROJ] = win_own[...]
-    wout[pl.ds(pl.multiple_of(shard * (INNER // shards), 16), INNER // shards), :] = wout_own[...]
-    s["parts"][shard] = sm_own[...]
+    own = wout.at[pl.ds(pl.multiple_of(shard * (INNER // shards), 16), INNER // shards), :]
+    fetch = pltpu.make_async_copy(wout_own, own, s["mixed_sem"])
+    fetch.start()
+    s["parts"][shard] = sm_own[0:8, :]
+    fetch.wait()
+    hd[0:2, :] = sm_own[8:10, :128]
     greet(at, shards)
     sems = (send_sems, recv_sems)
     conv_part = Gather(at, win, shards, MODEL // shards, INNER, (PADDED - INNER) // 2, sems, 0)
@@ -747,11 +770,6 @@
         small(d).start()
     conv_part.begin()
     setup(seg_ref, s)
-    conv_part.spread()
-    gate_part.begin()
-    out_part.begin()
-    conv_part.relay()
-    conv_part.share()
     for d in range(1, shards):
         small(d).wait_recv()
         small(d).wait_send()
@@ -759,16 +777,18 @@
     taps = spread_lanes(s["parts"], 448, 448)
     gain = spread_lanes(s["parts"], 384, 384)
     first = spread_lanes(s["parts"], 192, 192)
-    sm[...] = jnp.where(row < 5, taps, jnp.where(row == 5, gain, first))
-    sm[7:8, :] = hd[2:3, :]
+    sm[0:8, :] = jnp.where(row < 5, taps, jnp.where(row == 5, gain, first))
+    skip = packed(jnp.broadcast_to(sm_own[10:11, :128], (8, 128)))
+    sm[7:8, :INNER] = nn(skip, s["one64"][...])[0:1, :]
+    conv_part.spread()
+    norm_input(0, x_ref, sm, s)
+    conv_part.relay()
+    norm_input(1, x_ref, sm, s)
+    conv_part.share()
+    gate_part.begin()
+    out_part.begin()
     conv_part.finish()
-    for part in (gate_part, out_part):
-        part.spread()
-        part.relay()
-        part.share()
-    for part in (gate_part, out_part):
-        part.finish()
-    return at
+    return at, gate_part, out_part
 
 
 def copy_weights(seg_ref, win_all, wout_all, sm_all, hd, s, sems):
@@ -781,7 +801,9 @@
     setup(seg_ref, s)
     for copy in copies:
         copy.wait()
-    s["sm"][7:8, :] = hd[2:3, :]
+    hd[0:2, :] = s["sm"][8:10, :128]
+    skip = packed(jnp.broadcast_to(s["sm"][10:11, :128], (8, 128)))
+    s["sm"][7:8, :INNER] = nn(skip, s["one64"][...])[0:1, :]
 
 
 def transposed(src, dst):
@@ -819,22 +841,31 @@
 
 
 def pack_small(mine, s):
+    high, low = two_parts(s["acc"][7, :, :INNER])
+    skip = nn(high, s["sum64"][...]) + nn(low, s["sum64"][...])
+    s["acc"][7, :, 0:128] = skip
+    heads = [jnp.sum(s["acc"][k, :, 0:128], axis=0, keepdims=True) for k in (7, 8, 9)] + [jnp.zeros((1, 128), f32)]
     for j in range(CONV_CH // 256):
-        sums = [jnp.sum(s["acc"][k, :, j * 256 : (j + 1) * 256], axis=0, keepdims=True) for k in range(10)]
-        mine[0, j * 16 : (j + 1) * 16, :] = jnp.concatenate(sums + [jnp.zeros((6, 256), f32)], axis=0)
+        sums = [jnp.sum(s["acc"][k, :, j * 256 : (j + 1) * 256], axis=0, keepdims=True) for k in range(6)]
+        tail = jnp.concatenate(heads[2 * j : 2 * j + 2], axis=1) if j < 2 else jnp.zeros((1, 256), f32)
+        mine[0, j * 8 : (j + 1) * 8, :] = jnp.concatenate(sums + [tail, jnp.zeros((1, 256), f32)], axis=0)
+
+
+def pack_gain(mine, s):
+    sums = [jnp.sum(s["acc"][6, :, j * 128 : (j + 1) * 128], axis=0, keepdims=True) for j in range(MODEL // 128)]
+    mine[0] = jnp.concatenate(sums + [jnp.zeros((2, 128), f32)], axis=0)
 
 
 def layer_kernel(
-    direct, shards, x_ref, cot_ref, seg_ref, win_own, wout_own, sm_own, hd, mixed_ref, gtok_ref, gin_ref, gout_ref, gsm_ref, *refs
+    direct, shards, x_ref, cot_ref, seg_ref, win_own, wout_own, sm_own, mixed_ref, gtok_ref, gin_ref, gout_ref, gsm_ref, *refs
 ):
     s = dict(zip(SCRATCH, refs))
     s["mixed_sem"], *sems = refs[len(SCRATCH) :]
-    s["y"] = gtok_ref
     s["part"] = s["z"]
-    win, wout, sm = s["win"], s["wout"], s["sm"]
+    win, wout, sm, hd = s["win"], s["wout"], s["sm"], s["hd"]
     if direct:
         *sems, sends, recvs, locals_, total_send, total_recv, forward_done, scan_done = sems
-        at = gather_weights(shards, seg_ref, win_own, wout_own, sm_own, hd, s, *sems)
+        at, gate_part, out_part = gather_weights(shards, x_ref, seg_ref, win_own, wout_own, sm_own, hd, s, *sems)
         pair = (sends, recvs)
         zr, xbc, dy = s["zr"], s["xbc"], s["dy"]
         gate_sum = Reduce(
@@ -843,26 +874,69 @@
         out_sum = Reduce(
             at, s["dwo"], INNER, MODEL // 2, [(wout, 0, 0), (wout, 0, 384), (wout, 768, 384), (wout, 1152, 384)], gout_ref, 0, pair, 1, locals_.at[1]
         )
-        conv_sum = Reduce(
-            at, s["dwu"], MODEL, 1024, [(xbc, 0, 0), (dy, 0, 0), (dy, 384, 0), (dy, 576, 0)], gin_ref, INNER, pair, 2, locals_.at[2]
+        early_sum, late_sum = (
+            Reduce(
+                at,
+                s["dwu"].at[:, i * 1024 : (i + 1) * 1024],
+                MODEL,
+                512,
+                [(xbc, 0, i * 512), (dy, 0, i * 512), (dy, 384, i * 512), (dy, 576, i * 512)],
+                gin_ref,
+                INNER + i * 1024,
+                pair,
+                2 + i,
+                locals_.at[2 + i],
+            )
+            for i in range(2)
         )
-        small_sum = Total(at, s["mine"], s["up"], (total_send, total_recv))
+        totals = (total_send, total_recv)
+        small_sum = Total(
+            at, s["mine"], lambda i: s["up"].at[i // 3, pl.ds(8 + (i % 3) * 56, 56), :], totals, 0
+        )
+        gain_sum = Total(at, s["gain"], lambda i: s["gain_slots"].at[i], totals, 1)
     else:
         copy_weights(seg_ref, win_own, wout_own, sm_own, hd, s, *sems)
+        for q in range(SEQ):
+            norm_input(q, x_ref, sm, s)
     chunks = LEN // CHUNK
 
     @pl.loop(0, SEQ)
     def _(q):
-        project(q, x_ref, seg_ref, win, sm, hd, s)
+        project(q, win, sm, hd, s)
         s["state"][...] = jnp.zeros((STATE, INNER), f32)
+        if direct:
+
+            @pl.when(q == 0)
+            def _():
+                gate_part.spread()
+                out_part.spread()
 
         @pl.loop(0, chunks)
         def _(c):
             scan_forward(q, c, seg_ref, sm, hd, s)
-
-        @pl.loop(0, LEN // 256)
-        def _(i):
-            gate(q, i, x_ref, cot_ref, win, wout, sm, mixed_ref, s)
+            if direct:
+                polls = ((2, gate_part.relay), (3, out_part.relay))
+                for index, poll in polls:
+
+                    @pl.when((q == 0) & (c == index))
+                    def _():
+                        poll()
+
+                @pl.when((q == 1) & (c == 0))
+                def _():
+                    gate_part.share()
+
+                @pl.when((q == 1) & (c == 1))
+                def _():
+                    out_part.share()
+
+    if direct:
+        gate_part.finish()
+        out_part.finish()
+
+    @pl.loop(0, TOKENS // 256)
+    def _(i):
+        gate(i, x_ref, cot_ref, win, wout, sm, mixed_ref, s)
 
     if direct:
         meet(at, shards, forward_done)
@@ -877,72 +951,111 @@
     if direct:
         gate_sum.begin()
 
-    @pl.loop(0, SEQ * chunks)
-    def _(n):
-        @pl.when(n % chunks == 0)
-        def _():
-            s["state"][...] = jnp.zeros((STATE, INNER), f32)
-
-        scan_backward(n // chunks, chunks - 1 - n % chunks, seg_ref, sm, hd, s)
-        if direct:
-            stages = ((0, "first"), (2, "second"), (4, "third"), (6, "fourth"), (7, "fifth"))
-            for index, name in stages:
+    def backward(quads, first, polls):
+        @pl.loop(0, SEQ * chunks)
+        def _(n):
+            @pl.when(n % chunks == 0)
+            def _():
+                s["state"][:, quads[0] * 256 : (quads[-1] + 1) * 256] = jnp.zeros((STATE, len(quads) * 256), f32)
+
+            scan_backward(n // chunks, chunks - 1 - n % chunks, quads, first, seg_ref, sm, hd, s)
+            for index, poll in polls:
 
                 @pl.when(n == index)
                 def _():
-                    getattr(out_sum, name)()
-                    getattr(gate_sum, name)()
-
+                    poll()
+
+    polls = ()
+    if direct:
+        polls = (
+            (0, out_sum.first),
+            (1, gate_sum.first),
+            (3, out_sum.second),
+            (5, out_sum.third),
+            (6, gate_sum.second),
+            (7, out_sum.fourth),
+        )
+    backward(range(4), True, polls)
     if direct:
         meet(at, shards, scan_done)
-        out_sum.sixth()
-        gate_sum.sixth()
 
     @pl.loop(0, SEQ)
     def _(q):
-        conv_backward(q, sm, s)
-
-    for j in range(CONV_CH // 256):
+        conv_backward(q, range(8), sm, s)
+
+    if direct:
+        gate_sum.third()
+    for j in range(4):
+        in_weight_gradient(s["dwu"], j * 256, s["u"].at[:, j * 256 : (j + 1) * 256])(turned)
+    if direct:
+        met(shards, scan_done)
+        early_sum.begin()
+        polls = (
+            (0, out_sum.sixth),
+            (1, early_sum.first),
+            (3, gate_sum.fourth),
+            (6, early_sum.second),
+            (7, gate_sum.sixth),
+        )
+    backward(range(4, QUADS), False, polls)
+
+    @pl.loop(0, SEQ)
+    def _(q):
+        conv_backward(q, range(8, CONV_CH // 128), sm, s)
+
+    for j in range(4, CONV_CH // 256):
         in_weight_gradient(s["dwu"], j * 256, s["u"].at[:, j * 256 : (j + 1) * 256])(turned)
     in_weight_gradient(s["dwu"], CONV_CH, s["ddt"])(turned)
     s["dwu"][:, CONV_CH + 128 :] = jnp.zeros((MODEL, 128), bf16)
-    if direct:
-        met(shards, scan_done)
-        conv_sum.begin()
-        token_gradient(0, win, gtok_ref, s)
-        conv_sum.first()
-
-        @pl.loop(1, TOKENS // 256)
-        def _(i):
-            token_gradient(i, win, gtok_ref, s)
-
-        conv_sum.second()
-    else:
-
-        @pl.loop(0, TOKENS // 256)
-        def _(i):
-            token_gradient(i, win, gtok_ref, s)
-
-    @pl.loop(0, TOKENS // 128)
+    pack_small(s["mine"], s)
+    if direct:
+        late_sum.begin()
+        small_sum.begin()
+        early_sum.third()
+        small_sum.step(0)
+
+    @pl.loop(0, TOKENS // 256)
+    def _(i):
+        token_gradient(i, win, gtok_ref, s)
+        if direct:
+
+            @pl.when(i == 0)
+            def _():
+                late_sum.first()
+
+            @pl.when(i == 1)
+            def _():
+                small_sum.step(1)
+
+            @pl.when(i == 3)
+            def _():
+                small_sum.step(2)
+
+    if direct:
+        early_sum.fourth()
+
+    @pl.loop(0, TOKENS // 64)
     def _(i):
         input_gradient(i, x_ref, cot_ref, sm, gtok_ref, s)
 
-    pack_small(s["mine"], s)
-    if direct:
-        small_sum.begin()
-        conv_sum.third()
-        small_sum.step(0)
+    pack_gain(s["gain"], s)
+    if direct:
+        gain_sum.begin()
+        late_sum.second()
+        gain_sum.step(0)
+        early_sum.sixth()
+        gain_sum.step(1)
+        late_sum.third()
+        gain_sum.step(2)
         out_sum.seventh()
         gate_sum.seventh()
-        small_sum.step(1)
-        conv_sum.fourth()
-        small_sum.step(2)
-        conv_sum.fifth()
-        conv_sum.sixth()
-        small_sum.finish(gsm_ref)
-        conv_sum.seventh()
+        late_sum.fourth()
+        early_sum.seventh()
+        late_sum.sixth()
+        unpack_small(small_sum.finish(), gain_sum.finish(), gsm_ref)
+        late_sum.seventh()
     else:
-        gsm_ref[...] = s["mine"][0]
+        unpack_small(s["mine"][0], s["gain"][0], gsm_ref)
         copies = [
             pltpu.make_async_copy(s["dwz"], gin_ref.at[:, :INNER], sems[0].at[0]),
             pltpu.make_async_copy(s["dwu"], gin_ref.at[:, INNER:], sems[0].at[1]),
@@ -958,14 +1071,14 @@
     return mesh.shape["rep"] == 8 and mesh.shape["shard"] == 4
 
 
-def layer(mesh, x, cot, seg, win, wout, sm, hd):
+def layer(mesh, x, cot, seg, win, wout, sm):
     direct, shards = reaches(mesh), mesh.shape["shard"]
     vmem = pl.BlockSpec(memory_space=pltpu.VMEM)
     hbm = pl.BlockSpec(memory_space=pl.ANY)
     dma = pltpu.SemaphoreType.DMA
     if direct:
         sems = [dma((3, 5, shards)), dma((3, 5, shards)), dma((shards,)), dma((shards,))]
-        sems += [dma((3, 10)), dma((3, 10)), dma((3,)), dma((6,)), dma((6,))]
+        sems += [dma((4, 10)), dma((4, 10)), dma((4,)), dma((2, 6)), dma((2, 6))]
         sems += [pltpu.SemaphoreType.REGULAR] * 2
         options = dict(collective_id=0, has_side_effects=True)
         weights = vmem
@@ -978,45 +1091,40 @@
             jax.ShapeDtypeStruct((TOKENS, MODEL), f32),
             jax.ShapeDtypeStruct((MODEL // shards if direct else MODEL, PADDED), bf16),
             jax.ShapeDtypeStruct((INNER // shards if direct else INNER, MODEL), bf16),
-            jax.ShapeDtypeStruct((112, 256), f32),
+            jax.ShapeDtypeStruct((16, CONV_CH), f32),
         ),
-        in_specs=[vmem] * 3 + [weights] * 3 + [vmem],
+        in_specs=[vmem] * 3 + [weights, hbm, weights],
         out_specs=[hbm, vmem, hbm, hbm, vmem],
         scratch_shapes=[pltpu.VMEM(shape, kind) for shape, kind in SCRATCH.values()] + [dma] + sems,
         compiler_params=pltpu.CompilerParams(vmem_limit_bytes=67043328, **options),
         name="layer",
-    )(x, cot, seg, win, wout, sm, hd)
-
-
-def rows_to_lanes(v, width):
-    return jnp.pad(v.astype(f32), (0, width - v.shape[0]))[None]
+    )(x, cot, seg, win, wout, sm)
+
+
+def placed(v, row, width):
+    return jnp.pad(v.astype(f32), ((row, 16 - row - v.shape[0]), (0, width - v.shape[1])))
 
 
 def on_device(mesh, tokens, segment_ids, norm_gain, in_weight, conv_weight, conv_bias, dt_bias, a_log, d_skip, gate_gain, out_weight, cotangent):
-    small = (conv_bias, gate_gain, norm_gain)
+    small, heads = (conv_bias, gate_gain, norm_gain), (dt_bias, a_log, d_skip)
     if reaches(mesh):
-        win, wout = in_weight, out_weight
-        sm = jnp.concatenate([conv_weight.T.astype(f32)] + [rows_to_lanes(v, 512 - 64) for v in small + (norm_gain,)])
-        sm = jnp.pad(sm, ((0, 0), (0, 64)))
+        win, wout, taps, width = in_weight, out_weight, conv_weight, 512
     else:
         win, wout, taps, *small = lax.all_gather(
             (in_weight, out_weight, conv_weight) + small, "shard", axis=0, tiled=True
         )
-        win = jnp.pad(win, ((0, 0), (0, PADDED - PROJ)))
-        sm = jnp.concatenate([taps.T.astype(f32)] + [rows_to_lanes(v, CONV_CH) for v in (*small, small[-1])])
-    hd = jnp.concatenate(
-        [rows_to_lanes(v, CONV_CH) for v in (dt_bias, a_log, jnp.repeat(d_skip, HEADDIM))] + [jnp.zeros((5, CONV_CH), f32)],
-        axis=0,
-    )
+        win, width = jnp.pad(win, ((0, 0), (0, PADDED - PROJ))), CONV_CH
+    sm = placed(taps.T, 0, width)
+    for row, v in enumerate((*small, jnp.zeros((1,), f32), *heads)):
+        sm = sm + placed(v[None], CONV + row, width)
     mixed, gtok, gin, gout, gsm = layer(
         mesh,
-        tokens.reshape(TOKENS, MODEL), cotangent.reshape(TOKENS, MODEL), segment_ids, win, wout, sm, hd
+        tokens.reshape(TOKENS, MODEL), cotangent.reshape(TOKENS, MODEL), segment_ids, win, wout, sm
     )
     if not reaches(mesh):
         gin = lax.psum(lax.psum_scatter(gin, "shard", scatter_dimension=0, tiled=True), "rep")
         gout = lax.psum(lax.psum_scatter(gout, "shard", scatter_dimension=0, tiled=True), "rep")
         gsm = lax.psum(gsm, ("rep", "shard"))
-    gsm = gsm.reshape(CONV_CH // 256, 16, 256).transpose(1, 0, 2).reshape(16, CONV_CH)
     me = lax.axis_index("shard")
 
     def owned(v, like):
@@ -1031,7 +1139,7 @@
         owned(gsm[4], conv_bias),
         gsm[8, :HEADS],
         gsm[9, :HEADS],
-        gsm[7, :INNER].reshape(HEADS, HEADDIM).sum(axis=1),
+        gsm[7, :HEADS],
         owned(gsm[5, :INNER], gate_gain),
         gout.astype(f32),
     )

time: 237 us -> 197 us (0.83)
  Pallas kernels: 215 us -> 176 us
    pallas_call x1, Pallas kernels: 215 us -> 176 us  [layer(): pl.pallas_call(partial(layer_kernel, direct, shards), out_shape=(jax.Shap...]
    pad x5 -> x0, local copies, waits for them, and re-layouts: 2.67 us -> none  [rows_to_lanes(): return jnp.pad(v.astype(f32), (0, width - v.shape[0]))[None]]
    unnamed x11 -> x8, local copies, waits for them, and re-layouts: 5.79 us -> 4.86 us
where the time goes in v3:
time: 197 us
  Pallas kernels  176 us (89%)
  local copies, waits for them, and re-layouts  13.9 us (7%)
  other arithmetic  5.52 us (3%)
    pallas_call x1, Pallas kernels, layer(): pl.pallas_call(partial(layer_kernel, direct, shards), out_shape=(jax.Shap...  176 us
    unnamed x8, local copies, waits for them, and re-layouts  4.86 us

profile of v3, /device:TPU:0, one launch (start us, length us, event | category | flops | bytes accessed | tf_op | source)
XLA Modules:
  0.0 196.5 jit_solution(3783285424817847503)
XLA Ops:
  0.6 0.7 convert_element_type.39
  1.3 0.7 convert_element_type.40
  2.0 0.7 convert_element_type.41
  2.7 1.4 pad_add_fusion.sm_own
  4.0 176.4 %layer.1 = (bf16[1024,768]{1,0:T(8,128)(2,1)}, f32[1024,768]{1,0:T(8,128)}, bf16[192,3584]{1,0:T(8,128)(2,1)}, bf16[384,768]{1,0:T(8,128)(2,1)}, f32[16,1792]{1,0:T(8,128)}) custom-call(bf16[1024,768]{1,0:T(8,128)(2,1)} %bitcast.20, bf16[1024,768]{1,0:T(8,128)(2,1)} %bitcast.21, s32[2,512]{1,0:T(2,128)} %seg_ref.1, bf16[192,3352]{1,0:T(8,128)(2,1)} %win_own.1, ...), custom_call_target="tpu_custom_call" | custom-call | tf_op jit(solution)/shard_map/layer/pallas_call | solution.py:1087
  180.5 0.8 slice.26
  181.3 0.7 dynamic-slice_bitcast_fusion
  182.0 0.8 slice.27
  182.8 0.7 constant_dynamic-slice_fusion
  183.5 0.8 slice.31
  184.3 0.6 dynamic-slice_reduce_fusion
  184.9 0.7 slice.24
  185.6 0.6 constant_dynamic-slice_fusion.1
  186.2 1.3 slice_bitcast_fusion
  187.5 0.0 copy-start.2
  187.5 3.1 %slice_convert_fusion = f32[192,3352]{1,0:T(8,128)} fusion(bf16[192,3584]{1,0:T(8,128)(2,1)} %get-tuple-element.19), kind=kLoop, calls=%fused_computation | loop fusion | flops 643584 | bytes 3861504 | tf_op jit(solution)/shard_map/convert_element_type | solution.py:1137
  190.6 0.0 copy-start.1
  190.6 0.0 copy-done.2
  190.6 1.1 convert_element_type.43
  191.7 0.7 copy-done.1
  192.4 0.0 copy-start
  192.4 1.1 copy.25
  193.6 1.3 copy-done
  194.9 1.7 copy.26
Async XLA Ops:
  187.5 3.1 %copy-start.2 = (bf16[384,768]{1,0:T(8,128)(2,1)S(1)}, bf16[384,768]{1,0:T(8,128)(2,1)}, u32[]{:S(2)}) copy-start(bf16[384,768]{1,0:T(8,128)(2,1)} %get-tuple-element.20) | copy-start | bytes 1769476
  190.6 1.8 copy-start.1
  192.4 2.5 %copy-start = (f32[1024,768]{1,0:T(8,128)S(1)}, f32[1024,768]{1,0:T(8,128)}, u32[]{:S(2)}) copy-start(f32[1024,768]{1,0:T(8,128)} %get-tuple-element.17) | copy-start | bytes 9437188

commit v4 on v3

--- a/solution.py
+++ b/solution.py
@@ -1,4 +1,5 @@
 from functools import partial
+from types import SimpleNamespace
 
 import jax
 import jax.numpy as jnp
@@ -79,7 +80,7 @@
 
 
 def scanned(s, rows, cols):
-    return s["dy"][rows, cols].astype(f32) + s["dz"][rows, cols].astype(f32)
+    return s.dy[rows, cols].astype(f32) + s.dz[rows, cols].astype(f32)
 
 
 def place():
@@ -88,7 +89,7 @@
     px, py = (rep // 2) % 2, rep // 4
     a = px * (1 - core) + py * core
     b = py * (1 - core) + px * core
-    return dict(
+    return SimpleNamespace(
         rep=rep,
         shard=shard,
         core=core,
@@ -103,11 +104,11 @@
 
 def greet(at, shards):
     barrier = pltpu.get_barrier_semaphore()
-    for who in ("one", "two", "far", "mate"):
-        pl.semaphore_signal(barrier, inc=1, device_id=(at[who], at["shard"]), device_id_type=MESH)
+    for who in (at.one, at.two, at.far, at.mate):
+        pl.semaphore_signal(barrier, inc=1, device_id=(who, at.shard), device_id_type=MESH)
     for d in range(1, shards):
         pl.semaphore_signal(
-            barrier, inc=1, device_id=(at["rep"], (at["shard"] + d) % shards), device_id_type=MESH
+            barrier, inc=1, device_id=(at.rep, (at.shard + d) % shards), device_id_type=MESH
         )
     pl.semaphore_wait(barrier, 3 + shards)
 
@@ -124,7 +125,7 @@
         self.send, self.recv = (lambda kind, d: sems[0].at[part, kind, d]), (lambda kind, d: sems[1].at[part, kind, d])
 
     def columns(self):
-        return pl.ds(pl.multiple_of(self.start + self.at["core"] * self.half, 128), self.half)
+        return pl.ds(pl.multiple_of(self.start + self.at.core * self.half, 128), self.half)
 
     def piece(self, shard, a, b):
         tall = self.rows // 4
@@ -134,20 +135,20 @@
         return self.ref.at[pl.ds(pl.multiple_of(shard * self.rows, 16), self.rows), self.columns()]
 
     def source(self, d):
-        return (self.at["shard"] + self.shards - d) % self.shards
+        return (self.at.shard + self.shards - d) % self.shards
 
     def copy(self, kind, d):
         at = self.at
         if kind == 0:
-            own = self.piece(at["shard"], at["a"], at["b"])
-            return remote(own, own, self.send(0, d), self.recv(0, d), at["rep"], (at["shard"] + d) % self.shards)
+            own = self.piece(at.shard, at.a, at.b)
+            return remote(own, own, self.send(0, d), self.recv(0, d), at.rep, (at.shard + d) % self.shards)
         if kind == 4:
-            what, who = self.strip(self.source(d)), at["mate"]
+            what, who = self.strip(self.source(d)), at.mate
         elif kind == 3:
-            what, who = self.piece(self.source(d), at["a"], 1 - at["b"]), at["one"]
+            what, who = self.piece(self.source(d), at.a, 1 - at.b), at.one
         else:
-            what, who = self.piece(self.source(d), at["a"], at["b"]), at["one"] if kind == 1 else at["two"]
-        return remote(what, what, self.send(kind, d), self.recv(kind, d), who, at["shard"])
+            what, who = self.piece(self.source(d), at.a, at.b), at.one if kind == 1 else at.two
+        return remote(what, what, self.send(kind, d), self.recv(kind, d), who, at.shard)
 
     def each(self):
         return range(1, self.shards)
@@ -181,10 +182,10 @@
 
 
 def meet(at, shards, sem):
-    for who in ("one", "two", "far", "mate"):
-        pl.semaphore_signal(sem, inc=1, device_id=(at[who], at["shard"]), device_id_type=MESH)
+    for who in (at.one, at.two, at.far, at.mate):
+        pl.semaphore_signal(sem, inc=1, device_id=(who, at.shard), device_id_type=MESH)
     for d in range(1, shards):
-        pl.semaphore_signal(sem, inc=1, device_id=(at["rep"], (at["shard"] + d) % shards), device_id_type=MESH)
+        pl.semaphore_signal(sem, inc=1, device_id=(at.rep, (at.shard + d) % shards), device_id_type=MESH)
 
 
 def met(shards, sem):
@@ -198,8 +199,8 @@
         self.tall, self.own_rows = rows // 16, rows // 4
         self.send, self.recv = (lambda i: sems[0].at[part, i]), (lambda i: sems[1].at[part, i])
         self.local = local
-        self.keep = pl.ds(pl.multiple_of(at["core"] * half, 128), half)
-        self.give = pl.ds(pl.multiple_of((1 - at["core"]) * half, 128), half)
+        self.keep = pl.ds(pl.multiple_of(at.core * half, 128), half)
+        self.give = pl.ds(pl.multiple_of((1 - at.core) * half, 128), half)
 
     def slot(self, level, start, count):
         ref, row, column = self.slots[level]
@@ -216,7 +217,7 @@
         return remote(src, dst, self.send(index), self.recv(index), rep, shard)
 
     def partner(self, name):
-        return self.at[name], self.at["shard"]
+        return name, self.at.shard
 
     def add(self, start, level, place_in_slot):
         rows = pl.ds(start, self.tall)
@@ -225,7 +226,7 @@
 
     def halves(self):
         whole = self.slot(0, 0, self.rows)
-        return self.to(self.grad.at[:, self.give], whole, 0, self.partner("mate"))
+        return self.to(self.grad.at[:, self.give], whole, 0, self.partner(self.at.mate))
 
     def begin(self):
         self.halves().start()
@@ -242,10 +243,10 @@
         for shard in range(4):
             for b in range(2):
                 self.to(
-                    self.block(shard, 1 - at["a"], b),
+                    self.block(shard, 1 - at.a, b),
                     self.slot(1, (2 * shard + b) * self.tall, self.tall),
                     1,
-                    self.partner("one"),
+                    self.partner(self.at.one),
                 ).start()
 
     def all_of(self, level, index, name):
@@ -254,52 +255,52 @@
 
     def second(self):
         at = self.at
-        self.all_of(1, 1, "one").wait_recv()
+        self.all_of(1, 1, self.at.one).wait_recv()
         for shard in range(4):
             for b in range(2):
-                self.add(self.at_block(shard, at["a"], b), 1, (2 * shard + b) * self.tall)
+                self.add(self.at_block(shard, at.a, b), 1, (2 * shard + b) * self.tall)
         for shard in range(4):
             self.to(
-                self.block(shard, at["a"], 1 - at["b"]),
+                self.block(shard, at.a, 1 - at.b),
                 self.slot(2, shard * self.tall, self.tall),
                 2,
-                self.partner("two"),
+                self.partner(self.at.two),
             ).start()
 
     def across(self, d):
         at = self.at
-        shard = (at["shard"] + d) % 4
+        shard = (at.shard + d) % 4
         return self.to(
-            self.block(shard, at["a"], at["b"]), self.slot(3, (d - 1) * self.tall, self.tall), 2 + d, (at["rep"], shard)
+            self.block(shard, at.a, at.b), self.slot(3, (d - 1) * self.tall, self.tall), 2 + d, (at.rep, shard)
         )
 
     def third(self):
         at = self.at
-        self.all_of(2, 2, "two").wait_recv()
+        self.all_of(2, 2, self.at.two).wait_recv()
         for shard in range(4):
-            self.add(self.at_block(shard, at["a"], at["b"]), 2, shard * self.tall)
+            self.add(self.at_block(shard, at.a, at.b), 2, shard * self.tall)
         for d in range(1, 4):
             self.across(d).start()
 
     def landed(self, a, b):
         rows = pl.ds(pl.multiple_of((2 * b + a) * self.tall, 16), self.tall)
-        return self.out.at[rows, pl.ds(pl.multiple_of(self.column + self.at["core"] * self.half, 128), self.half)]
+        return self.out.at[rows, pl.ds(pl.multiple_of(self.column + self.at.core * self.half, 128), self.half)]
 
     def spread(self, index):
         at = self.at
-        own = self.block(at["shard"], at["a"], at["b"])
-        return self.to(own, self.landed(at["a"], at["b"]), index, self.partner(("one", "two", "far")[index - 6]))
+        own = self.block(at.shard, at.a, at.b)
+        return self.to(own, self.landed(at.a, at.b), index, self.partner((at.one, at.two, at.far)[index - 6]))
 
     def home(self):
         at = self.at
-        own = self.block(at["shard"], at["a"], at["b"])
-        return pltpu.make_async_copy(own, self.landed(at["a"], at["b"]), self.local)
+        own = self.block(at.shard, at.a, at.b)
+        return pltpu.make_async_copy(own, self.landed(at.a, at.b), self.local)
 
     def fourth(self):
         at = self.at
         for d in range(1, 4):
             self.across(d).wait_recv()
-        rows = pl.ds(self.at_block(at["shard"], at["a"], at["b"]), self.tall)
+        rows = pl.ds(self.at_block(at.shard, at.a, at.b), self.tall)
         total = self.grad[rows, self.keep].astype(f32)
         for d in range(1, 4):
             total = total + self.slot(3, (d - 1) * self.tall, self.tall)[...].astype(f32)
@@ -309,8 +310,8 @@
         self.home().start()
 
     def strip(self):
-        columns = pl.ds(pl.multiple_of(self.column + self.at["core"] * self.half, 128), self.half)
-        return self.to(self.out.at[:, columns], self.out.at[:, columns], 9, self.partner("mate"))
+        columns = pl.ds(pl.multiple_of(self.column + self.at.core * self.half, 128), self.half)
+        return self.to(self.out.at[:, columns], self.out.at[:, columns], 9, self.partner(self.at.mate))
 
     def sixth(self):
         self.home().wait()
@@ -321,8 +322,8 @@
     def seventh(self):
         self.strip().wait_recv()
         self.halves().wait_send()
-        self.all_of(1, 1, "one").wait_send()
-        self.all_of(2, 2, "two").wait_send()
+        self.all_of(1, 1, self.at.one).wait_send()
+        self.all_of(2, 2, self.at.two).wait_send()
         for d in range(1, 4):
             self.across(d).wait_send()
         for index in (6, 7, 8):
@@ -347,9 +348,9 @@
     def copy(self, index):
         at = self.at
         if index < 3:
-            who = at[("mate", "one", "two")[index]], at["shard"]
+            who = (at.mate, at.one, at.two)[index], at.shard
         else:
-            who = at["rep"], (at["shard"] + index - 2) % 4
+            who = at.rep, (at.shard + index - 2) % 4
         return remote(self.mine.at[min(index, 3)], self.slot(index), self.send(index), self.recv(index), *who)
 
     def begin(self):
@@ -383,24 +384,24 @@
 def setup(seg_ref, s):
     r, c = rows_of((128, 256)), lanes_of((128, 256))
     for j in range(HEADS * 128 // 256):
-        s["one128"][:, j * 256 : (j + 1) * 256] = (
+        s.one128[:, j * 256 : (j + 1) * 256] = (
             ((r & 31) == ((c + j * 256) >> 7)) & (r < 96)
         ).astype(f32).astype(bf16)
     for j in range(QUADS):
-        s["one64"][:, j * 256 : (j + 1) * 256] = (
+        s.one64[:, j * 256 : (j + 1) * 256] = (
             ((r & 31) == ((c + j * 256) >> 6)) & (r < 96)
         ).astype(f32).astype(bf16)
     r, c = rows_of((256, 128)), lanes_of((256, 128))
     for j in range(QUADS):
-        s["sum64"][j * 256 : (j + 1) * 256, :] = (((r + j * 256) >> 6) == c).astype(f32).astype(bf16)
-    s["acc"][...] = jnp.zeros(s["acc"].shape, f32)
-    s["pre"][TOKENS:, :] = jnp.zeros((16, CONV_CH), bf16)
-    s["up"][:, 0:8, :] = jnp.zeros((2, 8, 256), f32)
+        s.sum64[j * 256 : (j + 1) * 256, :] = (((r + j * 256) >> 6) == c).astype(f32).astype(bf16)
+    s.acc[...] = jnp.zeros(s.acc.shape, f32)
+    s.pre[TOKENS:, :] = jnp.zeros((16, CONV_CH), bf16)
+    s.up[:, 0:8, :] = jnp.zeros((2, 8, 256), f32)
     for q in range(SEQ):
-        s["segc"][q, 0:8, :] = jnp.full((8, 128), -1.0, f32)
+        s.segc[q, 0:8, :] = jnp.full((8, 128), -1.0, f32)
         for i in range(LEN // 128):
             seg = seg_ref[q : q + 1, i * 128 : (i + 1) * 128].astype(f32)
-            s["segc"][q, 8 + i * 128 : 8 + (i + 1) * 128, :] = jnp.broadcast_to(seg, (128, 128)).T
+            s.segc[q, 8 + i * 128 : 8 + (i + 1) * 128, :] = jnp.broadcast_to(seg, (128, 128)).T
 
 
 def norm_input(q, x_ref, sm, s):
@@ -409,50 +410,50 @@
         rows = pl.ds(pl.multiple_of(q * LEN + i * 64, 64), 64)
         x = x_ref[rows, :].astype(f32)
         r = lax.rsqrt(jnp.mean(x * x, axis=1, keepdims=True) + EPS)
-        s["nrm"][rows, :] = (x * r * sm[6:7, :MODEL]).astype(bf16)
+        s.nrm[rows, :] = (x * r * sm[6:7, :MODEL]).astype(bf16)
 
 
 def project(q, win, sm, hd, s):
     row0 = pl.multiple_of(q * LEN, LEN)
-    seg = s["segc"][q, 8 : 8 + LEN, :]
+    seg = s.segc[q, 8 : 8 + LEN, :]
     place = rows_of((LEN, 128))
     for o in range(1, CONV):
-        s["back"][o - 1] = ((seg == pltpu.roll(seg, o, 0)) & (place >= o)).astype(f32)
+        s.back[o - 1] = ((seg == pltpu.roll(seg, o, 0)) & (place >= o)).astype(f32)
     rows = pl.ds(row0, LEN)
-    raw = nn(s["nrm"][rows, :], win[:, DT : DT + 128]) + hd[0:1, :]
-    s["dtx"][rows, :] = raw
+    raw = nn(s.nrm[rows, :], win[:, DT : DT + 128]) + hd[0:1, :]
+    s.dtx[rows, :] = raw
     for j in range(CONV_CH // 256):
         slot = j % 2
-        s["up"][slot, 8:, :] = nn(s["nrm"][rows, :], win[:, INNER + j * 256 : INNER + (j + 1) * 256])
+        s.up[slot, 8:, :] = nn(s.nrm[rows, :], win[:, INNER + j * 256 : INNER + (j + 1) * 256])
         for i in range(LEN // 128):
             for half in range(2):
                 c0 = j * 256 + half * 128
                 here = pl.ds(row0 + i * 128, 128)
-                block = s["up"][slot, i * 128 : i * 128 + 136, half * 128 : (half + 1) * 128]
+                block = s.up[slot, i * 128 : i * 128 + 136, half * 128 : (half + 1) * 128]
                 u = block[8:]
                 tap = lambda k: sm[k : k + 1, c0 : c0 + 128]
                 pre = sm[4:5, c0 : c0 + 128] + tap(3) * u
                 for o in range(1, CONV):
-                    same = s["back"][o - 1, i * 128 : (i + 1) * 128, :]
+                    same = s.back[o - 1, i * 128 : (i + 1) * 128, :]
                     pre = pre + tap(3 - o) * (pltpu.roll(block, o, 0)[8:] * same)
-                s["u"][here, c0 : c0 + 128] = u.astype(bf16)
-                s["pre"][here, c0 : c0 + 128] = pre.astype(bf16)
-                s["xbc"][here, c0 : c0 + 128] = (pre * sigmoid(pre)).astype(bf16)
+                s.u[here, c0 : c0 + 128] = u.astype(bf16)
+                s.pre[here, c0 : c0 + 128] = pre.astype(bf16)
+                s.xbc[here, c0 : c0 + 128] = (pre * sigmoid(pre)).astype(bf16)
 
 
 def chunk_terms(q, c, seg_ref, hd, s):
     row0 = pl.multiple_of(q * LEN + c * CHUNK, CHUNK)
     rows = pl.ds(row0, CHUNK)
-    raw = s["dtx"][rows, :]
+    raw = s.dtx[rows, :]
     dt = jnp.maximum(raw, 0.0) + jnp.log1p(jnp.exp(-jnp.abs(raw)))
     rate = -jnp.exp(hd[1:2, :]) * dt
     lower = (rows_of((CHUNK, CHUNK)) >= lanes_of((CHUNK, CHUNK))).astype(f32)
     cum = exact(lower, rate)
     source = cum - jnp.log(jnp.maximum(dt, 1e-37))
     start = 8 + c * CHUNK
-    segc = s["segc"][q, pl.ds(pl.multiple_of(start, 8), CHUNK), :]
+    segc = s.segc[q, pl.ds(pl.multiple_of(start, 8), CHUNK), :]
     segr = segc.T
-    before = s["segc"][q, pl.ds(pl.multiple_of(start - 8, 8), 8), :][7:8]
+    before = s.segc[q, pl.ds(pl.multiple_of(start - 8, 8), 8), :][7:8]
     last = segc[CHUNK - 1 : CHUNK]
     carry = (segc == before).astype(f32)
     tail = (segc == last).astype(f32)
@@ -467,41 +468,41 @@
     rows, raw, dt, rate, cum, source, segc, segr, grow, shrink, keep = chunk_terms(q, c, seg_ref, hd, s)
     t, k = rows_of((CHUNK, CHUNK)), lanes_of((CHUNK, CHUNK))
     bound = jnp.where((segc == segr) & (t >= k), 3e38, -1e30)
-    s["rowv"][...] = source.T
+    s.rowv[...] = source.T
     target = packed(cum)
     grow_p, shrink_p = packed(grow), packed(shrink)
     keep_p = packed(jnp.broadcast_to(keep, (8, 128)))
-    bv = s["xbc"][rows, INNER : INNER + STATE]
-    cv = s["xbc"][rows, INNER + STATE :]
+    bv = s.xbc[rows, INNER : INNER + STATE]
+    cv = s.xbc[rows, INNER + STATE :]
     gram = nt(cv, bv)
     bt = bv.T
     at = q * (LEN // CHUNK) + c
     left = lanes_of((CHUNK, 128)) < HEADDIM
     for j in range(QUADS):
         cols = slice(j * 256, (j + 1) * 256)
-        grow_e = nn(grow_p, s["one64"][:, cols])
-        shrink_e = nn(shrink_p, s["one64"][:, cols])
-        keep_e = nn(keep_p, s["one64"][:, cols])[0:1, :]
-        state = s["state"][:, cols]
+        grow_e = nn(grow_p, s.one64[:, cols])
+        shrink_e = nn(shrink_p, s.one64[:, cols])
+        keep_e = nn(keep_p, s.one64[:, cols])[0:1, :]
+        state = s.state[:, cols]
         low_state = state.astype(bf16)
-        s["states"][at, :, cols] = low_state
+        s.states[at, :, cols] = low_state
         y_state = nn(cv, low_state)
-        xv = s["xbc"][rows, cols]
+        xv = s.xbc[rows, cols]
         xw = (xv.astype(f32) * shrink_e).astype(bf16)
-        s["state"][:, cols] = state * keep_e + nn(bt, xw)
+        s.state[:, cols] = state * keep_e + nn(bt, xw)
         parts = []
         for pair in range(2):
-            spread = nn(target, s["one128"][:, j * 512 + pair * 256 : j * 512 + (pair + 1) * 256])
+            spread = nn(target, s.one128[:, j * 512 + pair * 256 : j * 512 + (pair + 1) * 256])
             weights = []
             for half in range(2):
                 head = 4 * j + 2 * pair + half
-                d = spread[:, half * 128 : (half + 1) * 128] - s["rowv"][head : head + 1, :]
+                d = spread[:, half * 128 : (half + 1) * 128] - s.rowv[head : head + 1, :]
                 weights.append((gram * jnp.exp(jnp.minimum(d, bound))).astype(bf16))
             x2 = xv[:, pair * 128 : (pair + 1) * 128]
             zero = jnp.zeros_like(x2)
             stack = jnp.concatenate([jnp.where(left, x2, zero), jnp.where(left, zero, x2)], axis=0)
             parts.append(nn(jnp.concatenate(weights, axis=1), stack))
-        s["dy"][rows, cols], s["dz"][rows, cols] = two_parts(jnp.concatenate(parts, axis=1) + y_state * grow_e)
+        s.dy[rows, cols], s.dz[rows, cols] = two_parts(jnp.concatenate(parts, axis=1) + y_state * grow_e)
 
 
 def gate(i, x_ref, cot_ref, win, wout, sm, mixed_ref, s):
@@ -510,8 +511,8 @@
     rows = pl.ds(pl.multiple_of(row0, tall), tall)
     for j in range(QUADS):
         cols = slice(j * 256, (j + 1) * 256)
-        s["z"][:, cols] = nn(s["nrm"][rows, :], win[:, cols])
-        s["dg"][:, cols] = nt(cot_ref[rows, :], wout[cols, :])
+        s.z[:, cols] = nn(s.nrm[rows, :], win[:, cols])
+        s.dg[:, cols] = nt(cot_ref[rows, :], wout[cols, :])
 
     @pl.loop(0, tall // block)
     def _(b):
@@ -521,51 +522,51 @@
         along = jnp.zeros((block, 128), f32)
         for j in range(INNER // 128):
             cols = slice(j * 128, (j + 1) * 128)
-            z = s["z"][own, cols]
-            y = scanned(s, where, cols) + sm[7:8, cols] * s["xbc"][where, cols].astype(f32)
+            z = s.z[own, cols]
+            y = scanned(s, where, cols) + sm[7:8, cols] * s.xbc[where, cols].astype(f32)
             v = y * (z * sigmoid(z))
             square = square + v * v
-            along = along + s["dg"][own, cols] * sm[5:6, cols] * v
+            along = along + s.dg[own, cols] * sm[5:6, cols] * v
         r = lax.rsqrt(jnp.sum(square, axis=1, keepdims=True) * (1.0 / INNER) + EPS)
         k = r * r * r * (jnp.sum(along, axis=1, keepdims=True) * (1.0 / INNER))
         for j in range(INNER // 128):
             cols = slice(j * 128, (j + 1) * 128)
-            z = s["z"][own, cols]
-            dg = s["dg"][own, cols]
+            z = s.z[own, cols]
+            dg = s.dg[own, cols]
             ys = scanned(s, where, cols)
-            xv = s["xbc"][where, cols].astype(f32)
+            xv = s.xbc[where, cols].astype(f32)
             y = ys + sm[7:8, cols] * xv
             sg = sigmoid(z)
             zs = z * sg
             v = y * zs
             vr = v * r
             gain = sm[5:6, cols]
-            s["gated"][where, cols] = (vr * gain).astype(bf16)
-            s["acc"][5, :, cols] += partial_sum(dg * vr)
+            s.gated[where, cols] = (vr * gain).astype(bf16)
+            s.acc[5, :, cols] += partial_sum(dg * vr)
             dv = r * (dg * gain) - v * k
             dy = dv * zs
             low_dy = dy.astype(bf16)
-            s["dy"][where, cols] = low_dy
-            s["dz"][where, cols] = (dv * y * (sg + zs * (1.0 - sg))).astype(bf16)
-            s["acc"][7, :, cols] += partial_sum(dy * xv)
-            s["dg"][own, cols] = low_dy.astype(f32) * ys
-
-    high, low = two_parts(s["dg"][...])
-    s["rowdot"][rows, :] = nn(high, s["sum64"][...]) + nn(low, s["sum64"][...])
-    branch = nn(s["gated"][rows, :], wout[...])
-    s["mixed"][...] = (x_ref[rows, :].astype(f32) + branch).astype(bf16)
-    out = pltpu.make_async_copy(s["mixed"], mixed_ref.at[rows, :], s["mixed_sem"])
+            s.dy[where, cols] = low_dy
+            s.dz[where, cols] = (dv * y * (sg + zs * (1.0 - sg))).astype(bf16)
+            s.acc[7, :, cols] += partial_sum(dy * xv)
+            s.dg[own, cols] = low_dy.astype(f32) * ys
+
+    high, low = two_parts(s.dg[...])
+    s.rowdot[rows, :] = nn(high, s.sum64[...]) + nn(low, s.sum64[...])
+    branch = nn(s.gated[rows, :], wout[...])
+    s.mixed[...] = (x_ref[rows, :].astype(f32) + branch).astype(bf16)
+    out = pltpu.make_async_copy(s.mixed, mixed_ref.at[rows, :], s.mixed_sem)
     out.start()
     out.wait()
 
 
 def set_aside(s, at, kind):
     row, column = (at // 4) * 128, ((at % 4) * 3 + kind) * 128
-    return s["dg"].at[pl.ds(pl.multiple_of(row, 128), 128), pl.ds(pl.multiple_of(column, 128), 128)]
+    return s.dg.at[pl.ds(pl.multiple_of(row, 128), 128), pl.ds(pl.multiple_of(column, 128), 128)]
 
 
 def sums_aside(s, at):
-    return s["z"].at[128:256, pl.ds(pl.multiple_of(at * 128, 128), 128)]
+    return s.z.at[128:256, pl.ds(pl.multiple_of(at * 128, 128), 128)]
 
 
 def scan_backward(q, c, quads, first, seg_ref, sm, hd, s):
@@ -573,12 +574,12 @@
     k, t = rows_of((CHUNK, CHUNK)), lanes_of((CHUNK, CHUNK))
     allowed = (segc == segr) & (t >= k)
     bound = jnp.where(allowed, 3e38, -1e30)
-    s["rowv"][...] = cum.T
+    s.rowv[...] = cum.T
     origin = packed(source)
     grow_p, shrink_p = packed(grow), packed(shrink)
     keep_p = packed(jnp.broadcast_to(keep, (8, 128)))
-    bv = s["xbc"][rows, INNER : INNER + STATE]
-    cv = s["xbc"][rows, INNER + STATE :]
+    bv = s.xbc[rows, INNER : INNER + STATE]
+    cv = s.xbc[rows, INNER + STATE :]
     gram = nt(bv, cv)
     ct = cv.T
     at = q * (LEN // CHUNK) + c
@@ -586,100 +587,100 @@
     dgram = jnp.zeros((CHUNK, CHUNK), f32) if first else set_aside(s, at, 0)[...]
     for j in quads:
         cols = slice(j * 256, (j + 1) * 256)
-        grow_e = nn(grow_p, s["one64"][:, cols])
-        s["dys"][:, cols] = (s["dy"][rows, cols].astype(f32) * grow_e).astype(bf16)
-        shrink_e = nn(shrink_p, s["one64"][:, cols])
-        s["xw"][:, cols] = (s["xbc"][rows, cols].astype(f32) * shrink_e).astype(bf16)
-        low_dstate = s["state"][:, cols].astype(bf16)
-        s["lowd"][:, cols] = low_dstate
+        grow_e = nn(grow_p, s.one64[:, cols])
+        s.dys[:, cols] = (s.dy[rows, cols].astype(f32) * grow_e).astype(bf16)
+        shrink_e = nn(shrink_p, s.one64[:, cols])
+        s.xw[:, cols] = (s.xbc[rows, cols].astype(f32) * shrink_e).astype(bf16)
+        low_dstate = s.state[:, cols].astype(bf16)
+        s.lowd[:, cols] = low_dstate
         part = nn(bv, low_dstate) * shrink_e
-        s["part"][:CHUNK, cols] = part
-        keep_e = nn(keep_p, s["one64"][:, cols])[0:1, :]
-        kept = s["state"][:, cols] * keep_e
-        s["tail"][:, cols] = partial_sum(s["xbc"][rows, cols].astype(f32) * part) + partial_sum(
-            kept * s["states"][at, :, cols].astype(f32)
+        s.part[:CHUNK, cols] = part
+        keep_e = nn(keep_p, s.one64[:, cols])[0:1, :]
+        kept = s.state[:, cols] * keep_e
+        s.tail[:, cols] = partial_sum(s.xbc[rows, cols].astype(f32) * part) + partial_sum(
+            kept * s.states[at, :, cols].astype(f32)
         )
-        s["state"][:, cols] = kept + nn(ct, s["dys"][:, cols])
+        s.state[:, cols] = kept + nn(ct, s.dys[:, cols])
     for j in range(2 * quads[0], 2 * quads[-1] + 2):
         cols = slice(j * 128, (j + 1) * 128)
-        xv = s["xbc"][rows, cols]
-        dy = s["dy"][rows, cols]
-        spread = nn(origin, s["one128"][:, j * 256 : (j + 1) * 256])
+        xv = s.xbc[rows, cols]
+        dy = s.dy[rows, cols]
+        spread = nn(origin, s.one128[:, j * 256 : (j + 1) * 256])
         zero = jnp.zeros_like(dy)
         stack = jnp.concatenate([jnp.where(left, dy, zero), jnp.where(left, zero, dy)], axis=0)
         dweights = nt(xv, stack)
         weights = []
         for half in range(2):
             head = 2 * j + half
-            d = s["rowv"][head : head + 1, :] - spread[:, half * 128 : (half + 1) * 128]
+            d = s.rowv[head : head + 1, :] - spread[:, half * 128 : (half + 1) * 128]
             e = jnp.exp(jnp.minimum(d, bound))
             weights.append((gram * e).astype(bf16))
             dgram = dgram + dweights[:, half * 128 : (half + 1) * 128] * e
-        dx = nn(jnp.concatenate(weights, axis=1), stack) + s["part"][:CHUNK, cols]
-        s["part"][:CHUNK, cols] = xv.astype(f32) * dx
+        dx = nn(jnp.concatenate(weights, axis=1), stack) + s.part[:CHUNK, cols]
+        s.part[:CHUNK, cols] = xv.astype(f32) * dx
         dx = dx + sm[7:8, cols] * dy.astype(f32)
-        pre = s["pre"][rows, cols].astype(f32)
+        pre = s.pre[rows, cols].astype(f32)
         sg = sigmoid(pre)
-        s["pre"][rows, cols] = (dx * (sg * (1.0 + pre * (1.0 - sg)))).astype(bf16)
+        s.pre[rows, cols] = (dx * (sg * (1.0 + pre * (1.0 - sg)))).astype(bf16)
     some = slice(quads[0] * 256, (quads[-1] + 1) * 256)
-    high, low = two_parts(s["part"][:CHUNK, some])
-    colsum = nn(high, s["sum64"][some, :]) + nn(low, s["sum64"][some, :])
-    high, low = two_parts(s["tail"][:, some])
-    dlast = nn(high, s["sum64"][some, :]) + nn(low, s["sum64"][some, :])
-    dc = nt(s["dys"][:, some], s["states"][at, :, some])
-    db = nt(s["xw"][:, some], s["lowd"][:, some])
+    high, low = two_parts(s.part[:CHUNK, some])
+    colsum = nn(high, s.sum64[some, :]) + nn(low, s.sum64[some, :])
+    high, low = two_parts(s.tail[:, some])
+    dlast = nn(high, s.sum64[some, :]) + nn(low, s.sum64[some, :])
+    dc = nt(s.dys[:, some], s.states[at, :, some])
+    db = nt(s.xw[:, some], s.lowd[:, some])
     if first:
         for index, value in enumerate((dgram, db, dc)):
             set_aside(s, at, index)[...] = value
         sums_aside(s, at)[...] = colsum
-        s["kept_last"][at] = dlast
+        s.kept_last[at] = dlast
         return
     db, dc, colsum = db + set_aside(s, at, 1)[...], dc + set_aside(s, at, 2)[...], colsum + sums_aside(s, at)[...]
-    dlast = jnp.sum(dlast + s["kept_last"][at], axis=0, keepdims=True)
+    dlast = jnp.sum(dlast + s.kept_last[at], axis=0, keepdims=True)
     low_dgram = dgram.astype(bf16)
     db = db + nn(low_dgram, cv)
     dc = dc + tn(low_dgram, bv)
     for index, d in ((0, db), (1, dc)):
         cols = slice(INNER + index * STATE, INNER + (index + 1) * STATE)
-        pre = s["pre"][rows, cols].astype(f32)
+        pre = s.pre[rows, cols].astype(f32)
         sg = sigmoid(pre)
-        s["pre"][rows, cols] = (d * (sg * (1.0 + pre * (1.0 - sg)))).astype(bf16)
-    dcum = s["rowdot"][rows, :] - colsum
+        s.pre[rows, cols] = (d * (sg * (1.0 + pre * (1.0 - sg)))).astype(bf16)
+    dcum = s.rowdot[rows, :] - colsum
     drate = exact(allowed.astype(f32), dcum) + dlast * (segc == segc[CHUNK - 1 : CHUNK]).astype(f32)
     sg = sigmoid(raw)
     ratio = jnp.where(dt > 1e-30, sg / jnp.maximum(dt, 1e-30), 1.0)
     draw = colsum * ratio - drate * jnp.exp(hd[1:2, :]) * sg
     draw = jnp.where(lanes_of((CHUNK, 128)) < HEADS, draw, 0.0)
-    s["ddt"][rows, :] = draw.astype(bf16)
-    s["acc"][8, :, 0:128] += partial_sum(draw)
-    s["acc"][9, :, 0:128] += partial_sum(drate * rate)
+    s.ddt[rows, :] = draw.astype(bf16)
+    s.acc[8, :, 0:128] += partial_sum(draw)
+    s.acc[9, :, 0:128] += partial_sum(drate * rate)
 
 
 def conv_backward(q, tiles, sm, s):
     row0 = pl.multiple_of(q * LEN, LEN)
     rows = pl.ds(row0, LEN)
-    seg = s["segc"][q, 8 : 8 + LEN, :]
+    seg = s.segc[q, 8 : 8 + LEN, :]
     place = rows_of((LEN, 128))
     for o in range(1, CONV):
-        s["back"][o - 1] = ((seg == pltpu.roll(seg, LEN - o, 0)) & (place < LEN - o)).astype(f32)
+        s.back[o - 1] = ((seg == pltpu.roll(seg, LEN - o, 0)) & (place < LEN - o)).astype(f32)
     for j in tiles:
         cols = slice(j * 128, (j + 1) * 128)
         sums = [jnp.zeros((8, 128), f32)] * 5
         for i in range(LEN // 128):
             here = pl.ds(row0 + i * 128, 128)
-            block = s["pre"][pl.ds(row0 + i * 128, 144), cols].astype(f32)
+            block = s.pre[pl.ds(row0 + i * 128, 144), cols].astype(f32)
             ds = block[:128]
-            u = s["u"][here, cols].astype(f32)
+            u = s.u[here, cols].astype(f32)
             du = sm[3:4, cols] * ds
             sums[4] = sums[4] + partial_sum(ds)
             sums[3] = sums[3] + partial_sum(ds * u)
             for o in range(1, CONV):
-                moved = pltpu.roll(block, 144 - o, 0)[:128] * s["back"][o - 1, i * 128 : (i + 1) * 128, :]
+                moved = pltpu.roll(block, 144 - o, 0)[:128] * s.back[o - 1, i * 128 : (i + 1) * 128, :]
                 du = du + sm[3 - o : 4 - o, cols] * moved
                 sums[3 - o] = sums[3 - o] + partial_sum(moved * u)
-            s["u"][here, cols] = du.astype(bf16)
+            s.u[here, cols] = du.astype(bf16)
         for k in range(5):
-            s["acc"][k, :, cols] += sums[k]
+            s.acc[k, :, cols] += sums[k]
 
 
 def input_gradient(i, x_ref, cot_ref, sm, gtok_ref, s):
@@ -687,7 +688,7 @@
     x = x_ref[rows, :].astype(f32)
     dn = gtok_ref[rows, :]
     r = lax.rsqrt(jnp.mean(x * x, axis=1, keepdims=True) + EPS)
-    s["acc"][6, :, 0:MODEL] += partial_sum(dn * (x * r))
+    s.acc[6, :, 0:MODEL] += partial_sum(dn * (x * r))
     h = dn * sm[6:7, :MODEL]
     k = r * r * r * jnp.mean(h * x, axis=1, keepdims=True)
     gtok_ref[rows, :] = r * h - k * x + cot_ref[rows, :].astype(f32)
@@ -738,16 +739,16 @@
 
 
 def gather_weights(shards, x_ref, seg_ref, win_own, wout_own, sm_own, hd, s, send_sems, recv_sems, small_send, small_recv):
-    win, wout, sm = s["win"], s["wout"], s["sm"]
+    win, wout, sm = s.win, s.wout, s.sm
     at = place()
-    shard = at["shard"]
+    shard = at.shard
     rows = pl.ds(pl.multiple_of(shard * (MODEL // shards), 16), MODEL // shards)
     win[rows, DT:] = jnp.zeros((MODEL // shards, PADDED - DT), bf16)
     win[rows, :PROJ] = win_own[...]
     own = wout.at[pl.ds(pl.multiple_of(shard * (INNER // shards), 16), INNER // shards), :]
-    fetch = pltpu.make_async_copy(wout_own, own, s["mixed_sem"])
+    fetch = pltpu.make_async_copy(wout_own, own, s.mixed_sem)
     fetch.start()
-    s["parts"][shard] = sm_own[0:8, :]
+    s.parts[shard] = sm_own[0:8, :]
     fetch.wait()
     hd[0:2, :] = sm_own[8:10, :128]
     greet(at, shards)
@@ -758,11 +759,11 @@
 
     def small(d):
         return remote(
-            s["parts"].at[shard],
-            s["parts"].at[shard],
+            s.parts.at[shard],
+            s.parts.at[shard],
             small_send.at[d],
             small_recv.at[d],
-            at["rep"],
+            at.rep,
             (shard + d) % shards,
         )
 
@@ -774,12 +775,12 @@
         small(d).wait_recv()
         small(d).wait_send()
     row = rows_of((8, CONV_CH))
-    taps = spread_lanes(s["parts"], 448, 448)
-    gain = spread_lanes(s["parts"], 384, 384)
-    first = spread_lanes(s["parts"], 192, 192)
+    taps = spread_lanes(s.parts, 448, 448)
+    gain = spread_lanes(s.parts, 384, 384)
+    first = spread_lanes(s.parts, 192, 192)
     sm[0:8, :] = jnp.where(row < 5, taps, jnp.where(row == 5, gain, first))
     skip = packed(jnp.broadcast_to(sm_own[10:11, :128], (8, 128)))
-    sm[7:8, :INNER] = nn(skip, s["one64"][...])[0:1, :]
+    sm[7:8, :INNER] = nn(skip, s.one64[...])[0:1, :]
     conv_part.spread()
     norm_input(0, x_ref, sm, s)
     conv_part.relay()
@@ -793,17 +794,17 @@
 
 def copy_weights(seg_ref, win_all, wout_all, sm_all, hd, s, sems):
     copies = [
-        pltpu.make_async_copy(src, s[name], sems.at[i])
-        for i, (src, name) in enumerate(((win_all, "win"), (wout_all, "wout"), (sm_all, "sm")))
+        pltpu.make_async_copy(src, dst, sems.at[i])
+        for i, (src, dst) in enumerate(((win_all, s.win), (wout_all, s.wout), (sm_all, s.sm)))
     ]
     for copy in copies:
         copy.start()
     setup(seg_ref, s)
     for copy in copies:
         copy.wait()
-    hd[0:2, :] = s["sm"][8:10, :128]
-    skip = packed(jnp.broadcast_to(s["sm"][10:11, :128], (8, 128)))
-    s["sm"][7:8, :INNER] = nn(skip, s["one64"][...])[0:1, :]
+    hd[0:2, :] = s.sm[8:10, :128]
+    skip = packed(jnp.broadcast_to(s.sm[10:11, :128], (8, 128)))
+    s.sm[7:8, :INNER] = nn(skip, s.one64[...])[0:1, :]
 
 
 def transposed(src, dst):
@@ -817,7 +818,7 @@
 def out_weight_gradient(cot_ref, s):
     for j in range(QUADS):
         cols = slice(j * 256, (j + 1) * 256)
-        s["dwo"][cols, :] = tn(s["gated"][:, cols], cot_ref[...]).astype(bf16)
+        s.dwo[cols, :] = tn(s.gated[:, cols], cot_ref[...]).astype(bf16)
 
 
 def in_weight_gradient(ref, column, tile):
@@ -834,50 +835,50 @@
     for j in range(3):
         cols = slice(j * 256, (j + 1) * 256)
         gtok_ref[rows, cols] = (
-            nt(s["dz"][rows, :], win[cols, :INNER])
-            + nt(s["u"][rows, :], win[cols, INNER:DT])
-            + nt(s["ddt"][rows, :], win[cols, DT : DT + 128])
+            nt(s.dz[rows, :], win[cols, :INNER])
+            + nt(s.u[rows, :], win[cols, INNER:DT])
+            + nt(s.ddt[rows, :], win[cols, DT : DT + 128])
         )
 
 
 def pack_small(mine, s):
-    high, low = two_parts(s["acc"][7, :, :INNER])
-    skip = nn(high, s["sum64"][...]) + nn(low, s["sum64"][...])
-    s["acc"][7, :, 0:128] = skip
-    heads = [jnp.sum(s["acc"][k, :, 0:128], axis=0, keepdims=True) for k in (7, 8, 9)] + [jnp.zeros((1, 128), f32)]
+    high, low = two_parts(s.acc[7, :, :INNER])
+    skip = nn(high, s.sum64[...]) + nn(low, s.sum64[...])
+    s.acc[7, :, 0:128] = skip
+    heads = [jnp.sum(s.acc[k, :, 0:128], axis=0, keepdims=True) for k in (7, 8, 9)] + [jnp.zeros((1, 128), f32)]
     for j in range(CONV_CH // 256):
-        sums = [jnp.sum(s["acc"][k, :, j * 256 : (j + 1) * 256], axis=0, keepdims=True) for k in range(6)]
+        sums = [jnp.sum(s.acc[k, :, j * 256 : (j + 1) * 256], axis=0, keepdims=True) for k in range(6)]
         tail = jnp.concatenate(heads[2 * j : 2 * j + 2], axis=1) if j < 2 else jnp.zeros((1, 256), f32)
         mine[0, j * 8 : (j + 1) * 8, :] = jnp.concatenate(sums + [tail, jnp.zeros((1, 256), f32)], axis=0)
 
 
 def pack_gain(mine, s):
-    sums = [jnp.sum(s["acc"][6, :, j * 128 : (j + 1) * 128], axis=0, keepdims=True) for j in range(MODEL // 128)]
+    sums = [jnp.sum(s.acc[6, :, j * 128 : (j + 1) * 128], axis=0, keepdims=True) for j in range(MODEL // 128)]
     mine[0] = jnp.concatenate(sums + [jnp.zeros((2, 128), f32)], axis=0)
 
 
 def layer_kernel(
     direct, shards, x_ref, cot_ref, seg_ref, win_own, wout_own, sm_own, mixed_ref, gtok_ref, gin_ref, gout_ref, gsm_ref, *refs
 ):
-    s = dict(zip(SCRATCH, refs))
-    s["mixed_sem"], *sems = refs[len(SCRATCH) :]
-    s["part"] = s["z"]
-    win, wout, sm, hd = s["win"], s["wout"], s["sm"], s["hd"]
+    s = SimpleNamespace(**dict(zip(SCRATCH, refs)))
+    s.mixed_sem, *sems = refs[len(SCRATCH) :]
+    s.part = s.z
+    win, wout, sm, hd = s.win, s.wout, s.sm, s.hd
     if direct:
         *sems, sends, recvs, locals_, total_send, total_recv, forward_done, scan_done = sems
         at, gate_part, out_part = gather_weights(shards, x_ref, seg_ref, win_own, wout_own, sm_own, hd, s, *sems)
         pair = (sends, recvs)
-        zr, xbc, dy = s["zr"], s["xbc"], s["dy"]
+        zr, xbc, dy = s.zr, s.xbc, s.dy
         gate_sum = Reduce(
-            at, s["dwz"], MODEL, INNER // 2, [(zr, 0, 0), (zr, 768, 0), (zr, 1152, 0), (zr, 1344, 0)], gin_ref, 0, pair, 0, locals_.at[0]
+            at, s.dwz, MODEL, INNER // 2, [(zr, 0, 0), (zr, 768, 0), (zr, 1152, 0), (zr, 1344, 0)], gin_ref, 0, pair, 0, locals_.at[0]
         )
         out_sum = Reduce(
-            at, s["dwo"], INNER, MODEL // 2, [(wout, 0, 0), (wout, 0, 384), (wout, 768, 384), (wout, 1152, 384)], gout_ref, 0, pair, 1, locals_.at[1]
+            at, s.dwo, INNER, MODEL // 2, [(wout, 0, 0), (wout, 0, 384), (wout, 768, 384), (wout, 1152, 384)], gout_ref, 0, pair, 1, locals_.at[1]
         )
         early_sum, late_sum = (
             Reduce(
                 at,
-                s["dwu"].at[:, i * 1024 : (i + 1) * 1024],
+                s.dwu.at[:, i * 1024 : (i + 1) * 1024],
                 MODEL,
                 512,
                 [(xbc, 0, i * 512), (dy, 0, i * 512), (dy, 384, i * 512), (dy, 576, i * 512)],
@@ -891,9 +892,9 @@
         )
         totals = (total_send, total_recv)
         small_sum = Total(
-            at, s["mine"], lambda i: s["up"].at[i // 3, pl.ds(8 + (i % 3) * 56, 56), :], totals, 0
+            at, s.mine, lambda i: s.up.at[i // 3, pl.ds(8 + (i % 3) * 56, 56), :], totals, 0
         )
-        gain_sum = Total(at, s["gain"], lambda i: s["gain_slots"].at[i], totals, 1)
+        gain_sum = Total(at, s.gain, lambda i: s.gain_slots.at[i], totals, 1)
     else:
         copy_weights(seg_ref, win_own, wout_own, sm_own, hd, s, *sems)
         for q in range(SEQ):
@@ -903,7 +904,7 @@
     @pl.loop(0, SEQ)
     def _(q):
         project(q, win, sm, hd, s)
-        s["state"][...] = jnp.zeros((STATE, INNER), f32)
+        s.state[...] = jnp.zeros((STATE, INNER), f32)
         if direct:
 
             @pl.when(q == 0)
@@ -944,10 +945,10 @@
     if direct:
         met(shards, forward_done)
         out_sum.begin()
-    turned = s["gated"]
-    transposed(s["nrm"], turned)
+    turned = s.gated
+    transposed(s.nrm, turned)
     for j in range(QUADS):
-        in_weight_gradient(s["dwz"], j * 256, s["dz"].at[:, j * 256 : (j + 1) * 256])(turned)
+        in_weight_gradient(s.dwz, j * 256, s.dz.at[:, j * 256 : (j + 1) * 256])(turned)
     if direct:
         gate_sum.begin()
 
@@ -956,7 +957,7 @@
         def _(n):
             @pl.when(n % chunks == 0)
             def _():
-                s["state"][:, quads[0] * 256 : (quads[-1] + 1) * 256] = jnp.zeros((STATE, len(quads) * 256), f32)
+                s.state[:, quads[0] * 256 : (quads[-1] + 1) * 256] = jnp.zeros((STATE, len(quads) * 256), f32)
 
             scan_backward(n // chunks, chunks - 1 - n % chunks, quads, first, seg_ref, sm, hd, s)
             for index, poll in polls:
@@ -986,7 +987,7 @@
     if direct:
         gate_sum.third()
     for j in range(4):
-        in_weight_gradient(s["dwu"], j * 256, s["u"].at[:, j * 256 : (j + 1) * 256])(turned)
+        in_weight_gradient(s.dwu, j * 256, s.u.at[:, j * 256 : (j + 1) * 256])(turned)
     if direct:
         met(shards, scan_done)
         early_sum.begin()
@@ -1004,10 +1005,10 @@
         conv_backward(q, range(8, CONV_CH // 128), sm, s)
 
     for j in range(4, CONV_CH // 256):
-        in_weight_gradient(s["dwu"], j * 256, s["u"].at[:, j * 256 : (j + 1) * 256])(turned)
-    in_weight_gradient(s["dwu"], CONV_CH, s["ddt"])(turned)
-    s["dwu"][:, CONV_CH + 128 :] = jnp.zeros((MODEL, 128), bf16)
-    pack_small(s["mine"], s)
+        in_weight_gradient(s.dwu, j * 256, s.u.at[:, j * 256 : (j + 1) * 256])(turned)
+    in_weight_gradient(s.dwu, CONV_CH, s.ddt)(turned)
+    s.dwu[:, CONV_CH + 128 :] = jnp.zeros((MODEL, 128), bf16)
+    pack_small(s.mine, s)
     if direct:
         late_sum.begin()
         small_sum.begin()
@@ -1038,7 +1039,7 @@
     def _(i):
         input_gradient(i, x_ref, cot_ref, sm, gtok_ref, s)
 
-    pack_gain(s["gain"], s)
+    pack_gain(s.gain, s)
     if direct:
         gain_sum.begin()
         late_sum.second()
@@ -1055,11 +1056,11 @@
         unpack_small(small_sum.finish(), gain_sum.finish(), gsm_ref)
         late_sum.seventh()
     else:
-        unpack_small(s["mine"][0], s["gain"][0], gsm_ref)
+        unpack_small(s.mine[0], s.gain[0], gsm_ref)
         copies = [
-            pltpu.make_async_copy(s["dwz"], gin_ref.at[:, :INNER], sems[0].at[0]),
-            pltpu.make_async_copy(s["dwu"], gin_ref.at[:, INNER:], sems[0].at[1]),
-            pltpu.make_async_copy(s["dwo"], gout_ref, sems[0].at[2]),
+            pltpu.make_async_copy(s.dwz, gin_ref.at[:, :INNER], sems[0].at[0]),
+            pltpu.make_async_copy(s.dwu, gin_ref.at[:, INNER:], sems[0].at[1]),
+            pltpu.make_async_copy(s.dwo, gout_ref, sems[0].at[2]),
         ]
         for copy in copies:
             copy.start()

time: 197 us -> 197 us (level)
  no operation moved by 1% of the time
where the time goes in v4:
time: 197 us
  Pallas kernels  176 us (89%)
  local copies, waits for them, and re-layouts  13.9 us (7%)
  other arithmetic  5.52 us (3%)
    pallas_call x1, Pallas kernels, layer(): pl.pallas_call(partial(layer_kernel, direct, shards), out_shape=(jax.Shap...  176 us
    unnamed x8, local copies, waits for them, and re-layouts  4.86 us

profile of v4, /device:TPU:0, one launch (start us, length us, event | category | flops | bytes accessed | tf_op | source)
XLA Modules:
  0.0 196.5 jit_solution(3783285424817847503)
XLA Ops:
  0.6 0.7 convert_element_type.39
  1.3 0.7 convert_element_type.40
  2.0 0.7 convert_element_type.41
  2.7 1.4 pad_add_fusion.sm_own
  4.0 176.4 %layer.1 = (bf16[1024,768]{1,0:T(8,128)(2,1)}, f32[1024,768]{1,0:T(8,128)}, bf16[192,3584]{1,0:T(8,128)(2,1)}, bf16[384,768]{1,0:T(8,128)(2,1)}, f32[16,1792]{1,0:T(8,128)}) custom-call(bf16[1024,768]{1,0:T(8,128)(2,1)} %bitcast.20, bf16[1024,768]{1,0:T(8,128)(2,1)} %bitcast.21, s32[2,512]{1,0:T(2,128)} %seg_ref.1, bf16[192,3352]{1,0:T(8,128)(2,1)} %win_own.1, ...), custom_call_target="tpu_custom_call" | custom-call | tf_op jit(solution)/shard_map/layer/pallas_call | solution.py:1088
  180.5 0.8 slice.26
  181.3 0.7 dynamic-slice_bitcast_fusion
  182.0 0.8 slice.27
  182.8 0.7 constant_dynamic-slice_fusion
  183.5 0.8 slice.31
  184.3 0.6 dynamic-slice_reduce_fusion
  184.9 0.7 slice.24
  185.6 0.6 constant_dynamic-slice_fusion.1
  186.2 1.3 slice_bitcast_fusion
  187.5 0.0 copy-start.2
  187.5 3.1 %slice_convert_fusion = f32[192,3352]{1,0:T(8,128)} fusion(bf16[192,3584]{1,0:T(8,128)(2,1)} %get-tuple-element.19), kind=kLoop, calls=%fused_computation | loop fusion | flops 643584 | bytes 3861504 | tf_op jit(solution)/shard_map/convert_element_type | solution.py:1138
  190.6 0.0 copy-start.1
  190.6 0.0 copy-done.2
  190.6 1.1 convert_element_type.43
  191.7 0.7 copy-done.1
  192.4 0.0 copy-start
  192.4 1.1 copy.25
  193.6 1.3 copy-done
  194.9 1.7 copy.26
Async XLA Ops:
  187.5 3.1 %copy-start.2 = (bf16[384,768]{1,0:T(8,128)(2,1)S(1)}, bf16[384,768]{1,0:T(8,128)(2,1)}, u32[]{:S(2)}) copy-start(bf16[384,768]{1,0:T(8,128)(2,1)} %get-tuple-element.20) | copy-start | bytes 1769476
  190.6 1.8 copy-start.1
  192.4 2.5 %copy-start = (f32[1024,768]{1,0:T(8,128)S(1)}, f32[1024,768]{1,0:T(8,128)}, u32[]{:S(2)}) copy-start(f32[1024,768]{1,0:T(8,128)} %get-tuple-element.17) | copy-start | bytes 9437188

commit v5 on v4

--- a/solution.py
+++ b/solution.py
@@ -1034,6 +1034,7 @@
 
     if direct:
         early_sum.fourth()
+        late_sum.second()
 
     @pl.loop(0, TOKENS // 64)
     def _(i):
@@ -1042,7 +1043,6 @@
     pack_gain(s.gain, s)
     if direct:
         gain_sum.begin()
-        late_sum.second()
         gain_sum.step(0)
         early_sum.sixth()
         gain_sum.step(1)

time: 197 us -> 199 us (1.010)
  Pallas kernels: 176 us -> 178 us
where the time goes in v5:
time: 199 us; the launch traced here: 198 us
  Pallas kernels  178 us (89%)
  local copies, waits for them, and re-layouts  13.9 us (7%)
  other arithmetic  5.52 us (3%)
    pallas_call x1, Pallas kernels, layer(): pl.pallas_call(partial(layer_kernel, direct, shards), out_shape=(jax.Shap...  178 us
    unnamed x8, local copies, waits for them, and re-layouts  4.86 us

profile of v5, /device:TPU:0, one launch (start us, length us, event | category | flops | bytes accessed | tf_op | source)
XLA Modules:
  0.0 198.5 jit_solution(8832784483178035452)
XLA Ops:
  0.6 0.7 convert_element_type.39
  1.3 0.7 convert_element_type.40
  2.0 0.7 convert_element_type.41
  2.7 1.4 pad_add_fusion.sm_own
  4.0 178.4 %layer.1 = (bf16[1024,768]{1,0:T(8,128)(2,1)}, f32[1024,768]{1,0:T(8,128)}, bf16[192,3584]{1,0:T(8,128)(2,1)}, bf16[384,768]{1,0:T(8,128)(2,1)}, f32[16,1792]{1,0:T(8,128)}) custom-call(bf16[1024,768]{1,0:T(8,128)(2,1)} %bitcast.20, bf16[1024,768]{1,0:T(8,128)(2,1)} %bitcast.21, s32[2,512]{1,0:T(2,128)} %seg_ref.1, bf16[192,3352]{1,0:T(8,128)(2,1)} %win_own.1, ...), custom_call_target="tpu_custom_call" | custom-call | tf_op jit(solution)/shard_map/layer/pallas_call | solution.py:1088
  182.5 0.8 slice.26
  183.3 0.7 dynamic-slice_bitcast_fusion
  183.9 0.8 slice.27
  184.8 0.7 constant_dynamic-slice_fusion
  185.4 0.8 slice.31
  186.2 0.6 dynamic-slice_reduce_fusion
  186.8 0.7 slice.24
  187.6 0.6 constant_dynamic-slice_fusion.1
  188.2 1.3 slice_bitcast_fusion
  189.5 0.0 copy-start.2
  189.5 3.1 %slice_convert_fusion = f32[192,3352]{1,0:T(8,128)} fusion(bf16[192,3584]{1,0:T(8,128)(2,1)} %get-tuple-element.19), kind=kLoop, calls=%fused_computation | loop fusion | flops 643584 | bytes 3861504 | tf_op jit(solution)/shard_map/convert_element_type | solution.py:1138
  192.5 0.0 copy-start.1
  192.5 0.0 copy-done.2
  192.5 1.1 convert_element_type.43
  193.6 0.7 copy-done.1
  194.4 0.0 copy-start
  194.4 1.1 copy.25
  195.5 1.3 copy-done
  196.8 1.7 copy.26
Async XLA Ops:
  189.5 3.1 %copy-start.2 = (bf16[384,768]{1,0:T(8,128)(2,1)S(1)}, bf16[384,768]{1,0:T(8,128)(2,1)}, u32[]{:S(2)}) copy-start(bf16[384,768]{1,0:T(8,128)(2,1)} %get-tuple-element.20) | copy-start | bytes 1769476
  192.5 1.8 copy-start.1
  194.4 2.5 %copy-start = (f32[1024,768]{1,0:T(8,128)S(1)}, f32[1024,768]{1,0:T(8,128)}, u32[]{:S(2)}) copy-start(f32[1024,768]{1,0:T(8,128)} %get-tuple-element.17) | copy-start | bytes 9437188
